TPU v7x, 32 devices: a whole 2x2x4 slice. The times are simulated.
32 devices in a mesh: rep: 2 (over y), gx: 16 (over z, x, core).
Axes of the slice: x: 2, y: 2, z: 4, core: 2. Of those that a mesh axis runs over, the one named last changes fastest.
Arguments:
- positions: float32 [3, 32768], P(None, ('rep', 'gx')), parts along dimension 1, may hold values from 0 to 8, as said below
- field: float32 [3, 32768], P(None, ('rep', 'gx')), parts along dimension 1, may hold values from -45 to 45
- inv_polar: float32 [32768], P(('rep', 'gx')), parts along dimension 0, may hold values from 2 to 8
- x_spline: float32 [2, 5, 32768], P(None, None, ('rep', 'gx')), parts along dimension 2, may hold values from -1 to 1, as said below
- yz_spline: float32 [4, 32768, 128], P(None, ('rep', 'gx')), parts along dimension 1, may hold values from -1 to 1, as said below
- tile_list: int32 [256, 7], P(('rep', 'gx')), parts along dimension 0, may hold values from 0 to 13, as said below
- tile_count: int32 [256], P(('rep', 'gx')), parts along dimension 0, may hold values from 1 to 7, as said below
Outputs:
- dipoles: float32 [3, 32768], P(None, ('rep', 'gx')), parts along dimension 1
- residual: float32 [3, 32768], P(None, ('rep', 'gx')), parts along dimension 1
There are 2 independent parts, one for each index of `rep`. A program takes and returns all parts, laid end to end along the dimension named above; each array names one. Nothing has to cross between parts.
Inputs may be any that keep to these rules, and one draw needn't show every extreme that they name: `positions`: the first coordinate of an atom of block b of its slab lies in [b, b + 1); the other two lie in [0, 2). x_spline[0, k, i] and x_spline[1, k, i] are the cardinal B-spline of order 5 and its derivative at u_i + 4 - k for some u_i in [0, 1). `yz_spline`: rows 0 and 1 hold, for each atom, the cardinal B-spline of order 5 and its derivative at u + 4 - k placed at grid line (t + k) mod 128 for k < 5, for some start t and some u in [0, 1), and zero elsewhere; rows 2 and 3 likewise with their own start and offset. `tile_list`: row g = s * 8 + b lists in rising order the extended blocks b + 3 + e, -3 <= e <= 3, for which global blocks g and g + e (modulo 128) are neighbours; being neighbours is symmetric and always holds for e = 0; entries from tile_count[g] on equal b + 3. `tile_count`: global block 0 has all 7 neighbours.
All inputs are finite; a program needn't handle non-finite values.
Results may differ from a plain program's by a relative error of at most 0.0003.
Values sent between devices are 32-bit elements; how exact they have to be, the bound alone decides.
A program may use at most 64 MiB of HBM per device.

v0:
```python
import jax
import jax.numpy as jnp
from jax import lax
from jax.experimental import pallas as pl
from jax.experimental.pallas import tpu as pltpu
from jax.sharding import PartitionSpec as P
import functools
import numpy as np

GRID = 128
ORDER = 5
TILE = 128
HALO_BLK = 3
ITERS = 3


PAIR_C = 0.025
RECIP_C = 8192.0
DAMP = 0.0008
EXACT = lax.Precision.HIGHEST


def mode_of(freq, size):
    half_size = size // 2
    mode_num = jnp.where(freq <= half_size, freq, freq - half_size)
    weight = jnp.where((freq == 0) | (freq == half_size), 1.0 / size, 2.0 / size)
    return (mode_num.astype(jnp.float32), weight.astype(jnp.float32))


def basis_rows(size, points):
    freq = jnp.arange(size, dtype=jnp.int32)
    half_size = size // 2
    mode_num = jnp.where(freq <= half_size, freq, freq - half_size)
    phase = mode_num[:, None] * points[None, :] % size
    angle = phase.astype(jnp.float32) * (2.0 * jnp.pi / size)
    return jnp.where((freq <= half_size)[:, None], jnp.cos(angle), jnp.sin(angle))


def kernel_block(x_modes, x_weights, y_modes, y_weights, z_modes, z_weights):
    mode_sq = (
        x_modes[:, None, None] * x_modes[:, None, None]
        + y_modes[None, :, None] * y_modes[None, :, None]
        + z_modes[None, None, :] * z_modes[None, None, :]
    )
    safe_sq = jnp.where(mode_sq > 0, mode_sq, 1.0)
    green = jnp.where(mode_sq > 0, RECIP_C * jnp.exp(-DAMP * safe_sq) / safe_sq, 0.0)
    return green * x_weights[:, None, None] * y_weights[None, :, None] * z_weights[None, None, :]


F32 = jnp.float32
BF16 = jnp.bfloat16
VMEM = pl.BlockSpec(memory_space=pltpu.VMEM)


def split(x):
    high = x.astype(BF16)
    return high, (x - high.astype(F32)).astype(BF16)


def dot(a, b):
    return jnp.dot(a, b, preferred_element_type=F32)


def params(**more):
    return pltpu.CompilerParams(vmem_limit_bytes=56 * 1024 * 1024, **more)


def prep_kernel(yz_ref, rows_ref, yft_ref, zf_ref, zft_ref):
    rows = jnp.concatenate(split(rows_ref[...]), axis=0)

    def transformed(t):
        high, low = split(jnp.concatenate([yz_ref[t], yz_ref[t + 1]], axis=0))
        contract = (((1,), (1,)), ((), ()))
        wide = lax.dot_general(rows, high, contract, preferred_element_type=F32)
        more = lax.dot_general(rows[:GRID], low, contract, preferred_element_type=F32)
        return wide[:GRID] + wide[GRID:] + more

    lines = transformed(0)
    yft_ref[0, 0] = lines[:, :TILE]
    yft_ref[0, 1] = lines[:, TILE:]
    lines = transformed(2)
    zft_ref[0] = jnp.concatenate(split(lines), axis=0)
    zf_ref[0] = jnp.concatenate(split(lines.T), axis=1)


def prepare(yz_spline, rows, blocks):
    return pl.pallas_call(
        prep_kernel,
        grid=(blocks,),
        in_specs=[
            pl.BlockSpec((4, TILE, GRID), lambda b: (0, b, 0)),
            pl.BlockSpec((GRID, GRID), lambda b: (0, 0)),
        ],
        out_specs=[
            pl.BlockSpec((1, 2, GRID, TILE), lambda b: (b, 0, 0, 0)),
            pl.BlockSpec((1, 2 * TILE, 2 * GRID), lambda b: (b, 0, 0)),
            pl.BlockSpec((1, 2 * GRID, 2 * TILE), lambda b: (b, 0, 0)),
        ],
        out_shape=[
            jax.ShapeDtypeStruct((blocks, 2, GRID, TILE), F32),
            jax.ShapeDtypeStruct((blocks, 2 * TILE, 2 * GRID), BF16),
            jax.ShapeDtypeStruct((blocks, 2 * GRID, 2 * TILE), BF16),
        ],
        compiler_params=params(),
        name="prep",
    )(yz_spline, rows)


def spread_kernel(planes, ky_count, pv_ref, xs_ref, yft_ref, zf_ref, out_ref):
    blocks = pv_ref.shape[0]
    ranks = out_ref.shape[0]
    out_ref[...] = jnp.zeros_like(out_ref)

    def one_block(b, carry):
        base = b * planes // blocks
        y, dy = yft_ref[b, 0], yft_ref[b, 1]
        v0, v1, v2 = (pv_ref[b, 3 + c : 4 + c, :] for c in range(3))
        highs, lows = [], []
        for k in range(ORDER):
            x, dx = xs_ref[b, k : k + 1, :], xs_ref[b, ORDER + k : ORDER + k + 1, :]
            lead = (v0 * dx) * y + (v1 * x) * dy
            high, low = split(jnp.concatenate([lead, (v2 * x) * y], axis=1))
            highs.append(high)
            lows.append(low)
        weights = zf_ref[b]
        wide = dot(jnp.concatenate(highs, axis=0), weights)
        total = (
            wide[:, :GRID] + wide[:, GRID:] + dot(jnp.concatenate(lows, axis=0), weights[:, :GRID])
        )
        for k in range(ORDER):
            part = total[k * GRID : (k + 1) * GRID].reshape(ranks, ky_count, GRID)
            out_ref[:, base + k, :ky_count, :] += part
        return carry

    lax.fori_loop(0, blocks, one_block, 0)


def gather_kernel(
    planes, ky_count, ret_ref, xs_ref, yft_ref, zft_ref, pair_ref, pv_ref, polar_ref,
    next_ref, pv_next_ref, wide_ref, low_ref,
):
    blocks = xs_ref.shape[0]
    extent = ret_ref.shape[1]
    for p in range(extent):
        high, low = split(ret_ref[:, p, :ky_count, :].reshape(GRID, GRID))
        wide_ref[p] = jnp.concatenate([high, high], axis=1)
        low_ref[p] = low

    def one_block(b, carry):
        base = b * planes // blocks
        weights = zft_ref[b]
        wide = wide_ref[pl.ds(base, ORDER)].reshape(ORDER * GRID, 2 * GRID)
        low = low_ref[pl.ds(base, ORDER)].reshape(ORDER * GRID, GRID)
        sums = dot(wide, weights) + dot(low, weights[:GRID])
        one = two = three = 0.0
        for k in range(ORDER):
            x, dx = xs_ref[b, k : k + 1, :], xs_ref[b, ORDER + k : ORDER + k + 1, :]
            plain = sums[k * GRID : (k + 1) * GRID, :TILE]
            one += dx * plain
            two += x * plain
            three += x * sums[k * GRID : (k + 1) * GRID, TILE:]
        y, dy = yft_ref[b, 0], yft_ref[b, 1]
        far = jnp.concatenate(
            [jnp.sum(t, axis=0, keepdims=True) for t in (y * one, dy * two, y * three)], axis=0
        )
        following = pair_ref[b] - far
        next_ref[b] = following
        pv_next_ref[b, 0:3] = pv_ref[b, 0:3]
        pv_next_ref[b, 3:6] = following / polar_ref[b]
        pv_next_ref[b, 6:8] = jnp.zeros((2, TILE), F32)
        return carry

    lax.fori_loop(0, blocks, one_block, 0)


def pair_sum(near_ref, pv_ref, before_ref, after_ref, out_ref, ext_ref, col_ref):
    blocks = pv_ref.shape[0]
    reach = 2 * HALO_BLK + 1
    first_row = lax.broadcasted_iota(jnp.int32, (HALO_BLK, 8, TILE), 1) == 0
    ext_ref[:HALO_BLK] = before_ref[...] + jnp.where(first_row, -1.0 * blocks, 0.0)
    ext_ref[HALO_BLK : HALO_BLK + blocks] = pv_ref[...]
    ext_ref[HALO_BLK + blocks :] = after_ref[...] + jnp.where(first_row, 1.0 * blocks, 0.0)
    lag = lax.broadcasted_iota(jnp.int32, (8, TILE), 1) - lax.broadcasted_iota(
        jnp.int32, (8, TILE), 0
    )

    def spread_columns(e, carry):
        for c in range(6):
            col_ref[e, c] = jnp.broadcast_to(ext_ref[e, c : c + 1, :], (TILE, TILE)).T
        return carry

    lax.fori_loop(0, blocks + 2 * HALO_BLK, spread_columns, 0)

    def one_home(b, carry):
        home = [jnp.broadcast_to(pv_ref[b, c : c + 1, :], (8, TILE)) for c in range(3)]

        def one_source(k, sums):
            shift = jnp.where(k == HALO_BLK, 0, 4 * TILE)
            direct = [jnp.zeros((8, TILE), F32) for c in range(3)]
            tilted = [jnp.zeros((8, TILE), F32) for c in range(3)]
            for j in range(TILE // 8):
                rows = slice(8 * j, 8 * j + 8)
                r = [home[c] - col_ref[b + k, c, rows, :] for c in range(3)]
                v = [col_ref[b + k, 3 + c, rows, :] for c in range(3)]
                inverse = lax.rsqrt(r[0] * r[0] + r[1] * r[1] + r[2] * r[2] + 1.0)
                inverse = jnp.where(lag != 8 * j + shift, inverse, 0.0)
                square = inverse * inverse
                third = square * inverse
                weight = third * square * (r[0] * v[0] + r[1] * v[1] + r[2] * v[2])
                for c in range(3):
                    direct[c] += third * v[c]
                    tilted[c] += weight * r[c]
            near = near_ref[b * reach + k]
            return tuple(
                sums[c] + near * (direct[c] - 3.0 * tilted[c]) for c in range(3)
            )

        sums = lax.fori_loop(0, reach, one_source, (jnp.zeros((8, TILE), F32),) * 3)
        out_ref[b] = PAIR_C * jnp.concatenate(
            [jnp.sum(t, axis=0, keepdims=True) for t in sums], axis=0
        )
        return carry

    lax.fori_loop(0, blocks, one_home, 0)


def greet(ranks, me):
    barrier = pltpu.get_barrier_semaphore()

    def signal(d, carry):
        pl.semaphore_signal(
            barrier,
            inc=1,
            device_id={"gx": lax.rem(me + d, ranks)},
            device_id_type=pl.DeviceIdType.MESH,
        )
        return carry

    lax.fori_loop(1, ranks, signal, 0)
    pl.semaphore_wait(barrier, ranks - 1)


def exchange(ranks, me, source, target, local_sem, send_sem, recv_sem):
    def copy(d, slot):
        peer = lax.rem(me + d, ranks)
        return pltpu.make_async_remote_copy(
            src_ref=source(peer),
            dst_ref=target(slot),
            send_sem=send_sem.at[d],
            recv_sem=recv_sem.at[d],
            device_id={"gx": peer},
            device_id_type=pl.DeviceIdType.MESH,
        )

    def start(d, carry):
        copy(d, me).start()
        return carry

    def finish(d, carry):
        copy(d, lax.rem(me - d + ranks, ranks)).wait()
        return carry

    lax.fori_loop(1, ranks, start, 0)
    own = pltpu.make_async_copy(source(me), target(me), local_sem)
    own.start()

    def wait():
        own.wait()
        lax.fori_loop(1, ranks, finish, 0)

    return wait


def middle_kernel(
    ranks, ky_count, near_ref, spec_ref, pv_ref, green_ref, across_ref, back_ref,
    ret_ref, pair_ref,
    before_ref, after_ref, ext_ref, col_ref, recv_ref, done_ref, local_sems, send1, recv1, send2, recv2, halo_send, halo_recv,
):
    me = lax.axis_index("gx")
    blocks = pv_ref.shape[0]
    extent = spec_ref.shape[1]
    rows = ranks * extent
    greet(ranks, me)
    halos = []
    for t, (piece, into, step) in enumerate(
        (
            (pv_ref.at[pl.ds(blocks - HALO_BLK, HALO_BLK)], before_ref, 1),
            (pv_ref.at[pl.ds(0, HALO_BLK)], after_ref, ranks - 1),
        )
    ):
        halos.append(
            pltpu.make_async_remote_copy(
                src_ref=piece,
                dst_ref=into,
                send_sem=halo_send.at[t],
                recv_sem=halo_recv.at[t],
                device_id={"gx": lax.rem(me + step, ranks)},
                device_id_type=pl.DeviceIdType.MESH,
            )
        )
        halos[-1].start()
    wait = exchange(
        ranks, me, lambda d: spec_ref.at[d], lambda d: recv_ref.at[d], local_sems.at[0], send1, recv1
    )
    across_high, across_low = split(across_ref[...])
    back_high, back_low = split(back_ref[...])
    wait()
    lines_in = recv_ref.reshape(rows * 8, GRID)
    lines_out = done_ref.reshape(rows * 8, GRID)
    for q in range(ky_count):
        high, low = split(lines_in[pl.ds(q, rows, stride=8), :])
        wide = dot(across_high, jnp.concatenate([high, low], axis=1))
        line = wide[:, :GRID] + wide[:, GRID:] + dot(across_low, high)
        high, low = split(line * green_ref[q])
        wide = dot(back_high, jnp.concatenate([high, low], axis=1))
        lines_out[pl.ds(q, rows, stride=8), :] = (
            wide[:, :GRID] + wide[:, GRID:] + dot(back_low, high)
        )
    wait = exchange(
        ranks, me, lambda d: done_ref.at[d], lambda d: ret_ref.at[d], local_sems.at[1], send2, recv2
    )
    for halo in halos:
        halo.wait()
    pair_sum(near_ref, pv_ref, before_ref, after_ref, pair_ref, ext_ref, col_ref)
    wait()


def middle(near, spec, pv, green, across, back, ranks, ky_count):
    dma = pltpu.SemaphoreType.DMA
    blocks = pv.shape[0]
    halo = pltpu.VMEM((HALO_BLK, 8, TILE), F32)
    return pl.pallas_call(
        functools.partial(middle_kernel, ranks, ky_count),
        in_specs=[pl.BlockSpec(memory_space=pltpu.SMEM)] + [VMEM] * 5,
        out_specs=[VMEM] * 2,
        out_shape=[
            jax.ShapeDtypeStruct(spec.shape, F32),
            jax.ShapeDtypeStruct((blocks, 3, TILE), F32),
        ],
        scratch_shapes=[
            halo,
            halo,
            pltpu.VMEM((blocks + 2 * HALO_BLK, 8, TILE), F32),
            pltpu.VMEM((blocks + 2 * HALO_BLK, 6, TILE, TILE), F32),
            pltpu.VMEM(spec.shape, F32),
            pltpu.VMEM(spec.shape, F32),
            dma((2,)), dma((ranks,)), dma((ranks,)), dma((ranks,)), dma((ranks,)),
            dma((2,)), dma((2,)),
        ],
        compiler_params=params(collective_id=0, has_side_effects=True),
        name="middle",
    )(near, spec, pv, green, across, back)


def combine(weights, parts):
    terms = [w * p for w, p in zip(weights, parts) if w is not None]
    return functools.reduce(jnp.add, terms)


def scaled(a, x, y):
    pairs = zip(x, y)
    return [p if q is None else (a * q if p is None else p + a * q) for p, q in pairs]


def solve_kernel(
    ranks, b0_ref, b1_ref, b2_ref, b3_ref, polar_ref,
    dipoles_ref, residual_ref, part_ref, slots, local_sem, send_sem, recv_sem,
):
    me = lax.axis_index("gx")
    bases = [ref[...] for ref in (b0_ref, b1_ref, b2_ref, b3_ref)]
    soft = [b / polar_ref[...] for b in bases]
    count = ITERS + 1
    place = {}
    part_ref[...] = jnp.zeros_like(part_ref)
    for i in range(count):
        for j in range(i, count):
            place[i, j] = place[j, i] = row = len(set(place.values()))
            part_ref[row : row + 1] = jnp.sum(
                jnp.sum(bases[i] * soft[j], axis=0), axis=0, keepdims=True
            )
    greet(ranks, me)
    wait = exchange(
        ranks, me, lambda d: part_ref, lambda d: slots.at[d], local_sem.at[0], send_sem, recv_sem
    )
    wait()
    sums = jnp.sum(jnp.sum(slots[...], axis=0), axis=1, keepdims=True)
    sums = jnp.broadcast_to(sums, (sums.shape[0], TILE))

    def inner(x, y):
        value = None
        for i in range(count):
            for j in range(count):
                if x[i] is not None and y[j] is not None:
                    row = place[i, j]
                    term = x[i] * y[j] * sums[row : row + 1]
                    value = term if value is None else value + term
        return value

    none = [None] * (count - 1)
    residual = [jnp.ones((1, TILE), F32)] + none
    direction = list(residual)
    dipoles = [None] * count
    rz_now = inner(residual, residual)
    for sweep in range(ITERS):
        image = scaled(-1.0, direction, [None] + direction[:-1])
        step = rz_now / inner(direction, image)
        dipoles = scaled(step, dipoles, direction)
        residual = scaled(-step, residual, image)
        if sweep + 1 < ITERS:
            rz_next = inner(residual, residual)
            direction = scaled(rz_next / rz_now, residual, direction)
            rz_now = rz_next
    dipoles_ref[...] = combine(dipoles, soft)
    residual_ref[...] = combine(residual, bases)


def solve(bases, polar, ranks):
    dma = pltpu.SemaphoreType.DMA
    shape = bases[0].shape
    return pl.pallas_call(
        functools.partial(solve_kernel, ranks),
        in_specs=[VMEM] * 5,
        out_specs=[VMEM] * 2,
        out_shape=[jax.ShapeDtypeStruct(shape, F32)] * 2,
        scratch_shapes=[
            pltpu.VMEM((16, TILE), F32), pltpu.VMEM((ranks, 16, TILE), F32),
            dma((1,)), dma((ranks,)), dma((ranks,)),
        ],
        compiler_params=params(collective_id=1, has_side_effects=True),
        name="solve",
    )(*bases, polar)


def fixed_rows(points):
    half_size = GRID // 2
    freq = np.arange(GRID)
    mode_num = np.where(freq <= half_size, freq, freq - half_size)
    angle = (mode_num[:, None] * points[None, :] % GRID) * (2.0 * np.pi / GRID)
    return np.where((freq <= half_size)[:, None], np.cos(angle), np.sin(angle)).astype(np.float32)


def per_device(positions, field, inv_polar, x_spline, yz_spline, tile_list, tile_count):
    ranks = lax.axis_size("gx")
    rank_index = lax.axis_index("gx")
    atoms_here = positions.shape[1]
    planes = GRID // ranks
    extent = planes + 4
    blocks = atoms_here // TILE
    reach = 2 * HALO_BLK + 1
    ky_count = GRID // ranks

    def blocked(x):
        return x.reshape(-1, blocks, TILE).transpose(1, 0, 2)

    all_freq = jnp.arange(GRID, dtype=jnp.int32)
    fourier_rows = jnp.asarray(fixed_rows(np.arange(GRID)))
    ky_freq = rank_index * ky_count + jnp.arange(ky_count, dtype=jnp.int32)
    full_modes, full_weights = mode_of(all_freq, GRID)
    ky_modes, ky_weights = mode_of(ky_freq, GRID)
    green = kernel_block(ky_modes, ky_weights, full_modes, full_weights, full_modes, full_weights)
    source_rows = np.arange(ranks * extent)
    points = (source_rows // extent * planes - 2 + source_rows % extent) % GRID
    across = fixed_rows(points)
    back = jnp.asarray(np.ascontiguousarray(across.T))
    across = jnp.asarray(across)
    slots = jnp.arange(tile_list.shape[1], dtype=jnp.int32)
    wanted = jnp.arange(blocks, dtype=jnp.int32)[:, None] + jnp.arange(reach, dtype=jnp.int32)
    live = (slots[None, :] < tile_count[:, None])[:, :, None]
    near = jnp.any((tile_list[:, :, None] == wanted[:, None, :]) & live, axis=1)
    near = near.astype(F32).reshape(-1)
    yft, zf, zft = prepare(yz_spline, fourier_rows, blocks)
    xs = blocked(x_spline.reshape(2 * ORDER, atoms_here))
    pos = blocked(positions)
    polar = inv_polar.reshape(blocks, 1, TILE)
    spec_shape = jax.ShapeDtypeStruct((ranks, extent, 8, GRID), F32)
    rows_shape = jax.ShapeDtypeStruct((blocks, 3, TILE), F32)

    def advance(pv):
        spec = pl.pallas_call(
            functools.partial(spread_kernel, planes, ky_count),
            in_specs=[VMEM] * 4,
            out_specs=VMEM,
            out_shape=spec_shape,
            compiler_params=params(),
            name="spread",
        )(pv, xs, yft, zf)
        ret, pair = middle(near, spec, pv, green, across, back, ranks, ky_count)
        return pl.pallas_call(
            functools.partial(gather_kernel, planes, ky_count),
            in_specs=[VMEM] * 7,
            out_specs=[VMEM] * 2,
            out_shape=[rows_shape, jax.ShapeDtypeStruct((blocks, 8, TILE), F32)],
            scratch_shapes=[
                pltpu.VMEM((extent, GRID, 2 * GRID), BF16),
                pltpu.VMEM((extent, GRID, GRID), BF16),
            ],
            compiler_params=params(),
            name="gather",
        )(ret, xs, yft, zft, pair, pv, polar)

    bases = [blocked(field)]
    pv = jnp.concatenate([pos, bases[0] / polar, jnp.zeros((blocks, 2, TILE), F32)], axis=1)
    for sweep in range(ITERS):
        following, pv = advance(pv)
        bases.append(following)
    dipoles, residual = solve(bases, polar, ranks)

    def flat(x):
        return x.transpose(1, 0, 2).reshape(3, atoms_here)

    return flat(dipoles), flat(residual)


def solution(mesh):
    placed = (
        P(None, ("rep", "gx")),
        P(None, ("rep", "gx")),
        P(("rep", "gx")),
        P(None, None, ("rep", "gx")),
        P(None, ("rep", "gx"), None),
        P(("rep", "gx"), None),
        P(("rep", "gx")),
    )
    return jax.shard_map(
        per_device,
        mesh=mesh,
        in_specs=placed,
        out_specs=(P(None, ("rep", "gx")), P(None, ("rep", "gx"))),
        check_vma=False,
    )
```

profile of v0, /device:TPU:0, one launch (start us, length us, event | category | flops | bytes accessed | tf_op | source)
XLA Modules:
  0.0 193.8 jit_solution(18292863747286540626)
XLA Ops:
  0.6 0.1 pad.2.clone
  0.7 0.7 iota_compare_fusion
  1.4 0.1 broadcast_add_fusion
  1.5 0.8 copy.14
  2.2 0.1 and_reduce_fusion
  2.3 0.7 reshape.148.near_ref
  3.0 0.7 broadcast_divide_fusion
  3.7 1.4 maximum_maximum_fusion.pv_ref
  5.1 0.8 copy.15
  6.0 0.6 copy.18
  6.6 1.1 fusion.5.green_ref
  7.7 6.8 %prep.1 = (f32[8,2,128,128]{3,2,1,0:T(8,128)}, bf16[8,256,256]{2,1,0:T(8,128)(2,1)}, bf16[8,256,256]{2,1,0:T(8,128)(2,1)}) custom-call(f32[4,1024,128]{2,1,0:T(8,128)} %yz_ref.1, f32[128,128]{1,0:T(8,128)} %constant.14.clone.rows_ref), custom_call_target="tpu_custom_call" | custom-call | tf_op jit(solution)/shard_map/prep/pallas_call | solution.py:87
  14.5 5.3 %spread.3.spec_ref = f32[16,12,8,128]{3,2,1,0:T(8,128)} custom-call(f32[8,8,128]{2,1,0:T(8,128)} %maximum_maximum_fusion.pv_ref, f32[8,10,128]{2,1,0:T(8,128)} %bitcast.18, f32[8,2,128,128]{3,2,1,0:T(8,128)} %get-tuple-element.18.yft_ref, bf16[8,256,256]{2,1,0:T(8,128)(2,1)} %get-tuple-element.19.zf_ref), custom_call_target="tpu_custom_call" | custom-call | tf_op jit(solution)/shard_map/spread/pallas_call | solution.py:479
  19.8 40.3 %middle.3 = (f32[16,12,8,128]{3,2,1,0:T(8,128)}, f32[8,3,128]{2,1,0:T(4,128)}) custom-call(f32[56]{0:T(128)} %reshape.148.near_ref, f32[16,12,8,128]{3,2,1,0:T(8,128)} %spread.3.spec_ref, f32[8,8,128]{2,1,0:T(8,128)} %maximum_maximum_fusion.pv_ref, f32[8,128,128]{2,1,0:T(8,128)} %fusion.5.green_ref, f32[128,192]{1,0:T(8,128)} %constant.39.clone.across_ref, ...), custom_call_target="tpu_custom_call" | custom-call | tf_op jit(solution)/shard_map/middle/pallas_call | solution.py:332
  60.1 5.4 %gather.3 = (f32[8,3,128]{2,1,0:T(4,128)}, f32[8,8,128]{2,1,0:T(8,128)}) custom-call(f32[16,12,8,128]{3,2,1,0:T(8,128)} %get-tuple-element.20.ret_ref, f32[8,10,128]{2,1,0:T(8,128)} %bitcast.19, f32[8,2,128,128]{3,2,1,0:T(8,128)} %get-tuple-element.18.yft_ref, bf16[8,256,256]{2,1,0:T(8,128)(2,1)} %get-tuple-element.21.zft_ref, ...), custom_call_target="tpu_custom_call" | custom-call | tf_op jit(solution)/shard_map/gather/pallas_call | solution.py:488
  65.5 5.3 %spread.4.spec_ref = f32[16,12,8,128]{3,2,1,0:T(8,128)} custom-call(f32[8,8,128]{2,1,0:T(8,128)} %get-tuple-element.24.pv_ref, f32[8,10,128]{2,1,0:T(8,128)} %bitcast.20, f32[8,2,128,128]{3,2,1,0:T(8,128)} %get-tuple-element.18.yft_ref, bf16[8,256,256]{2,1,0:T(8,128)(2,1)} %get-tuple-element.19.zf_ref), custom_call_target="tpu_custom_call" | custom-call | tf_op jit(solution)/shard_map/spread/pallas_call | solution.py:479
  70.9 44.5 %middle.4 = (f32[16,12,8,128]{3,2,1,0:T(8,128)}, f32[8,3,128]{2,1,0:T(4,128)}) custom-call(f32[56]{0:T(128)} %reshape.148.near_ref, f32[16,12,8,128]{3,2,1,0:T(8,128)} %spread.4.spec_ref, f32[8,8,128]{2,1,0:T(8,128)} %get-tuple-element.24.pv_ref, f32[8,128,128]{2,1,0:T(8,128)} %fusion.5.green_ref, f32[128,192]{1,0:T(8,128)} %constant.39.clone.across_ref, ...), custom_call_target="tpu_custom_call" | custom-call | tf_op jit(solution)/shard_map/middle/pallas_call | solution.py:332
  115.4 5.4 %gather.4 = (f32[8,3,128]{2,1,0:T(4,128)}, f32[8,8,128]{2,1,0:T(8,128)}) custom-call(f32[16,12,8,128]{3,2,1,0:T(8,128)} %get-tuple-element.25.ret_ref, f32[8,10,128]{2,1,0:T(8,128)} %bitcast.21, f32[8,2,128,128]{3,2,1,0:T(8,128)} %get-tuple-element.18.yft_ref, bf16[8,256,256]{2,1,0:T(8,128)(2,1)} %get-tuple-element.21.zft_ref, ...), custom_call_target="tpu_custom_call" | custom-call | tf_op jit(solution)/shard_map/gather/pallas_call | solution.py:488
  120.8 5.3 %spread.5.spec_ref = f32[16,12,8,128]{3,2,1,0:T(8,128)} custom-call(f32[8,8,128]{2,1,0:T(8,128)} %get-tuple-element.28.pv_ref, f32[8,10,128]{2,1,0:T(8,128)} %bitcast.22, f32[8,2,128,128]{3,2,1,0:T(8,128)} %get-tuple-element.18.yft_ref, bf16[8,256,256]{2,1,0:T(8,128)(2,1)} %get-tuple-element.19.zf_ref), custom_call_target="tpu_custom_call" | custom-call | tf_op jit(solution)/shard_map/spread/pallas_call | solution.py:479
  126.1 44.4 %middle.5 = (f32[16,12,8,128]{3,2,1,0:T(8,128)}, f32[8,3,128]{2,1,0:T(4,128)}) custom-call(f32[56]{0:T(128)} %reshape.148.near_ref, f32[16,12,8,128]{3,2,1,0:T(8,128)} %spread.5.spec_ref, f32[8,8,128]{2,1,0:T(8,128)} %get-tuple-element.28.pv_ref, f32[8,128,128]{2,1,0:T(8,128)} %fusion.5.green_ref, f32[128,192]{1,0:T(8,128)} %constant.39.clone.across_ref, ...), custom_call_target="tpu_custom_call" | custom-call | tf_op jit(solution)/shard_map/middle/pallas_call | solution.py:332
  170.5 5.4 %gather.5 = (f32[8,3,128]{2,1,0:T(4,128)}, f32[8,8,128]{2,1,0:T(8,128)}) custom-call(f32[16,12,8,128]{3,2,1,0:T(8,128)} %get-tuple-element.29.ret_ref, f32[8,10,128]{2,1,0:T(8,128)} %bitcast.23, f32[8,2,128,128]{3,2,1,0:T(8,128)} %get-tuple-element.18.yft_ref, bf16[8,256,256]{2,1,0:T(8,128)(2,1)} %get-tuple-element.21.zft_ref, ...), custom_call_target="tpu_custom_call" | custom-call | tf_op jit(solution)/shard_map/gather/pallas_call | solution.py:488
  175.9 15.3 %solve.1 = (f32[8,3,128]{2,1,0:T(4,128)}, f32[8,3,128]{2,1,0:T(4,128)}) custom-call(f32[8,3,128]{2,1,0:T(4,128)} %bitcast.29, f32[8,3,128]{2,1,0:T(4,128)} %get-tuple-element.23.b1_ref, f32[8,3,128]{2,1,0:T(4,128)} %get-tuple-element.27.b2_ref, f32[8,3,128]{2,1,0:T(4,128)} %get-tuple-element.31.b3_ref, f32[8,1,128]{2,1,0:T(1,128)} %bitcast.28), custom_call_target="tpu_custom_call" | custom-call | tf_op jit(solution)/shard_map/solve/pallas_call | solution.py:420
  191.2 1.3 copy.21
  192.5 1.3 copy.22
  (6 shorter events, 0.0 us)
where the time goes:
time: 195 us; the launch traced here: 194 us
  Pallas kernels  183 us (94%)
  local copies, waits for them, and re-layouts  5.59 us (3%)
  other arithmetic  4.07 us (2%)
    pallas_call x3, Pallas kernels, middle(): pl.pallas_call(functools.partial(middle_kernel, ranks, ky_count), in_spec...  129 us
    pallas_call x3, Pallas kernels, advance(): pl.pallas_call(functools.partial(gather_kernel, planes, ky_count), in_spe...  16.2 us
    pallas_call x3, Pallas kernels, advance(): pl.pallas_call(functools.partial(spread_kernel, planes, ky_count), in_spe...  16 us
    pallas_call x1, Pallas kernels, solve(): pl.pallas_call(functools.partial(solve_kernel, ranks), in_specs=[VMEM] *...  15.3 us
    pallas_call x1, Pallas kernels, prepare(): pl.pallas_call(prep_kernel, grid=(blocks,), in_specs=[pl.BlockSpec((4, TI...  6.84 us
    unnamed x4, local copies, waits for them, and re-layouts  4.21 us

commit v1 on v0

--- a/solution.py
+++ b/solution.py
@@ -511,6 +511,600 @@
     return flat(dipoles), flat(residual)
 
 
+FIELD0 = 5
+
+
+def spline_rows(u):
+    v = 1.0 - u
+
+    def inner(p):
+        return ((((-4.0 * p + 4.0) * p + 6.0) * p + 4.0) * p + 1.0) * (1.0 / 24.0)
+
+    def slope(p):
+        return (((-4.0 * p + 3.0) * p + 3.0) * p + 1.0) * (1.0 / 6.0)
+
+    middle_value = ((((6.0 * u - 12.0) * u - 6.0) * u + 12.0) * u + 11.0) * (1.0 / 24.0)
+    middle_slope = (((2.0 * u - 3.0) * u - 1.0) * u + 1.0) * 0.5
+    values = [v * v * v * v * (1.0 / 24.0), inner(v), middle_value, inner(u), u * u * u * u * (1.0 / 24.0)]
+    slopes = [v * v * v * (-1.0 / 6.0), -slope(v), middle_slope, slope(u), u * u * u * (1.0 / 6.0)]
+    return values, slopes
+
+
+def turn(steps):
+    wrapped = steps - GRID * jnp.floor(steps * (1.0 / GRID) + 0.5)
+    half = wrapped * (np.pi / GRID)
+    square = half * half
+    sine = -1.0 / 39916800.0
+    for c in (1.0 / 362880.0, -1.0 / 5040.0, 1.0 / 120.0, -1.0 / 6.0, 1.0):
+        sine = sine * square + c
+    sine = sine * half
+    cosine = 1.0 / 479001600.0
+    for c in (-1.0 / 3628800.0, 1.0 / 40320.0, -1.0 / 720.0, 1.0 / 24.0, -0.5, 1.0):
+        cosine = cosine * square + c
+    return 1.0 - 2.0 * sine * sine, 2.0 * sine * cosine
+
+
+def iota(shape, dim):
+    return lax.broadcasted_iota(jnp.int32, shape, dim)
+
+
+CONTRACT_LANES = (((1,), (1,)), ((), ()))
+
+
+def fast_kernel(
+    ranks, pos_ref, field_ref, polar_ref, xs_ref, list_ref, count_ref,
+    center_ref, zin_ref, zout_ref, xin_ref, xout_ref, yz_ref,
+    dip_ref, res_ref,
+    lines, info, table, yq, xw, wt, vx, grid, spec, wide, low, green, tens, cols, place, sides, ext,
+    bases, pair, out_part, in_part, part, slots,
+    local_sem, ag_send, ag_recv, rs_send, rs_recv, side_send, side_recv, gram_send, gram_recv,
+):
+    me = lax.axis_index("gx")
+    blocks = polar_ref.shape[0]
+    planes = GRID // ranks
+    kys = GRID // ranks
+    halves = blocks // 4
+    reach = 2 * HALO_BLK + 1
+
+    def lanes(b):
+        return slice(b * TILE, (b + 1) * TILE)
+
+    loads = [
+        pltpu.make_async_copy(yz_ref.at[2 * t], lines.at[t], local_sem.at[t]) for t in range(2)
+    ]
+    for load in loads:
+        load.start()
+
+    barrier = pltpu.get_barrier_semaphore()
+
+    def greet_one(d, carry):
+        pl.semaphore_signal(
+            barrier, inc=1, device_id={"gx": lax.rem(me + d, ranks)}, device_id_type=pl.DeviceIdType.MESH
+        )
+        return carry
+
+    lax.fori_loop(1, ranks, greet_one, 0)
+
+    for c in range(3):
+        for b in range(blocks):
+            place[c, b : b + 1, :] = pos_ref[c : c + 1, lanes(b)]
+            bases[0, c, b : b + 1, :] = field_ref[c : c + 1, lanes(b)]
+    for c in range(3):
+        info[me, FIELD0 + c] = bases[0, c] / polar_ref[...]
+    offset = -1.5
+    for k in range(1, ORDER):
+        offset = offset + (1.0 * k) * xs_ref[k, 0:1, :]
+    for b in range(blocks):
+        info[me, 4, b : b + 1, :] = offset[:, lanes(b)]
+    for load in loads:
+        load.wait()
+    marks = iota((GRID, TILE), 0).astype(F32)
+    for t in range(2):
+        for b in range(blocks):
+            line = lines[t, lanes(b), :]
+            high = line.astype(BF16)
+            rest = line - high.astype(F32)
+            mid, tail = split(rest)
+            moment = lax.dot_general(
+                center_ref[...], jnp.concatenate([high, mid, tail], axis=1), CONTRACT_LANES,
+                preferred_element_type=F32,
+            )
+            moment, weight = moment[:GRID], moment[GRID:]
+            best = jnp.max(
+                jnp.where((jnp.abs(moment) < 0.5001) & (weight > 0.25), marks, -1.0), axis=0, keepdims=True
+            )
+            shift = jnp.sum(jnp.where(marks == best, moment, 0.0), axis=0, keepdims=True)
+            start = best - 2.0
+            info[me, 2 * t, b : b + 1, :] = jnp.where(start < 0, start + GRID, start)
+            info[me, 2 * t + 1, b : b + 1, :] = shift + 0.5
+
+    pl.semaphore_wait(barrier, ranks - 1)
+
+    def share(i, first, source=None):
+        owner = me if source is None else source
+        span = info.at[owner] if first else info.at[owner, pl.ds(FIELD0, 3)]
+        return pltpu.make_async_remote_copy(
+            src_ref=span, dst_ref=span, send_sem=ag_send.at[i], recv_sem=ag_recv.at[i],
+            device_id={"gx": lax.rem(me + i, ranks)}, device_id_type=pl.DeviceIdType.MESH,
+        )
+
+    def fold(i, slab):
+        return pltpu.make_async_remote_copy(
+            src_ref=out_part.at[slab], dst_ref=in_part.at[i], send_sem=rs_send.at[i], recv_sem=rs_recv.at[i],
+            device_id={"gx": slab}, device_id_type=pl.DeviceIdType.MESH,
+        )
+
+    def away(d):
+        step = (d + 1) // 2
+        return lax.rem(jnp.where(d % 2 == 1, step, ranks - step), ranks)
+
+    def start_share(first):
+        def one(d, carry):
+            share(away(d), first).start()
+            return carry
+
+        lax.fori_loop(1, ranks, one, 0)
+
+    def sent_share(first):
+        def one(i, carry):
+            share(i, first).wait_send()
+            return carry
+
+        lax.fori_loop(1, ranks, one, 0)
+
+    def got_share(d, first):
+        off = away(d)
+        share(lax.rem(ranks - off, ranks), first, lax.rem(me + off, ranks)).wait_recv()
+
+    start_share(True)
+    neighbours = [
+        pltpu.make_async_remote_copy(
+            src_ref=place, dst_ref=sides.at[t], send_sem=side_send.at[t], recv_sem=side_recv.at[t],
+            device_id={"gx": lax.rem(me + step, ranks)}, device_id_type=pl.DeviceIdType.MESH,
+        )
+        for t, step in enumerate((1, ranks - 1))
+    ]
+    for copy in neighbours:
+        copy.start()
+
+    def modes(freq):
+        number = jnp.where(freq <= GRID // 2, freq, freq - GRID // 2)
+        return number.astype(F32), jnp.where((freq == 0) | (freq == GRID // 2), 1.0 / GRID, 2.0 / GRID)
+
+    x_modes, x_weights = modes(iota((GRID, GRID), 0))
+    z_modes, z_weights = modes(iota((GRID, GRID), 1))
+    flat_sq = x_modes * x_modes + z_modes * z_modes
+    flat_weights = x_weights * z_weights
+
+    def filter_one(q, carry):
+        y_modes, y_weights = modes(jnp.full((GRID, GRID), me * kys + q, jnp.int32))
+        mode_sq = flat_sq + y_modes * y_modes
+        safe_sq = jnp.where(mode_sq > 0, mode_sq, 1.0)
+        value = jnp.where(mode_sq > 0, RECIP_C * jnp.exp(-DAMP * safe_sq) / safe_sq, 0.0)
+        green[q] = value * (flat_weights * y_weights)
+        return carry
+
+    lax.fori_loop(0, kys, filter_one, 0)
+
+    for copy in neighbours:
+        copy.wait()
+
+    def spread_columns(e, rows):
+        for c in range(3):
+            cols[e, c] = jnp.broadcast_to(rows[c], (TILE, TILE)).T
+
+    for e in range(blocks + 2 * HALO_BLK):
+        for c in range(3):
+            if e < HALO_BLK:
+                row = blocks - HALO_BLK + e
+                value = sides[0, c, row : row + 1, :] - (1.0 * blocks if c == 0 else 0.0)
+            elif e < HALO_BLK + blocks:
+                value = place[c, e - HALO_BLK : e - HALO_BLK + 1, :]
+            else:
+                row = e - HALO_BLK - blocks
+                value = sides[1, c, row : row + 1, :] + (1.0 * blocks if c == 0 else 0.0)
+            ext[e, c : c + 1, :] = value
+
+    def position_columns(e, carry):
+        spread_columns(e, [ext[e, c : c + 1, :] for c in range(3)])
+        return carry
+
+    lax.fori_loop(0, blocks + 2 * HALO_BLK, position_columns, 0)
+    lag = iota((8, TILE), 1) - iota((8, TILE), 0)
+
+    def tensors(index, carry):
+        b, k = index // reach, index % reach
+        near = jnp.float32(0.0)
+        for s in range(reach):
+            near = jnp.where((list_ref[b, s] == b + k) & (s < count_ref[b]), 1.0, near)
+        home = [jnp.broadcast_to(ext[b + HALO_BLK, c : c + 1, :], (8, TILE)) for c in range(3)]
+        hide = jnp.where(k == HALO_BLK, 0, 4 * TILE)
+        for j in range(TILE // 8):
+            rows = slice(8 * j, 8 * j + 8)
+            r = [home[c] - cols[b + k, c, rows, :] for c in range(3)]
+            inverse = lax.rsqrt(r[0] * r[0] + r[1] * r[1] + r[2] * r[2] + 1.0)
+            live = jnp.where(lag != 8 * j + hide, near, 0.0)
+            square = live * inverse * inverse
+            tens[index, 0, rows, :] = PAIR_C * (square * inverse)
+            weight = (3.0 * PAIR_C) ** 0.5 * (square * jnp.sqrt(inverse))
+            for c in range(3):
+                tens[index, 1 + c, rows, :] = weight * r[c]
+        return carry
+
+    lax.fori_loop(0, blocks * reach, tensors, 0)
+
+    freq = me * kys + iota((kys, TILE), 0)
+    sine_mode = freq > GRID // 2
+    number = jnp.where(sine_mode, freq - GRID // 2, freq).astype(F32)
+    lead_in = jnp.where(sine_mode, GRID // 4, 0).astype(F32)
+    shifts = [turn(number * (1.0 * k)) for k in range(ORDER)]
+
+    def slab_tables(d, carry):
+        @pl.when(d > 0)
+        def _():
+            got_share(d, True)
+
+        slab = lax.rem(me + away(d), ranks)
+        values, slopes = spline_rows(info[slab, 4])
+        for k in range(ORDER):
+            xw[slab, k] = values[k]
+            xw[slab, ORDER + k] = slopes[k]
+        for t in range(2):
+            values, slopes = spline_rows(info[slab, 2 * t + 1])
+            for k in range(ORDER):
+                wt[t, k] = values[k]
+                wt[t, ORDER + k] = slopes[k]
+
+        def block_tables(h, inner):
+            for j in range(4):
+                b = 4 * h + j
+
+                def row(t, k):
+                    return wt[t, k, pl.ds(b, 1), :]
+
+                first = jnp.broadcast_to(info[slab, 0, pl.ds(b, 1), :], (kys, TILE))
+                cosine, sine = turn(number * first - lead_in)
+                for t in range(2):
+                    real = combine([s[0] for s in shifts], [row(0, ORDER * t + k) for k in range(ORDER)])
+                    imag = combine([s[1] for s in shifts], [row(0, ORDER * t + k) for k in range(ORDER)])
+                    yq[slab * blocks + b, t] = cosine * real - sine * imag
+                begin = info[slab, 2, pl.ds(b, 1), :].astype(jnp.int32)
+                for i in range(GRID // 16):
+                    gap = (iota((16, TILE), 0) + (16 * i - begin)) & (GRID - 1)
+                    for t in range(2):
+                        dense = jnp.zeros((16, TILE), F32)
+                        for k in range(ORDER):
+                            dense = jnp.where(gap == k, row(1, ORDER * t + k), dense)
+                        high, rest = split(dense)
+                        at = slice((2 * j + t) * TILE, (2 * j + t + 1) * TILE)
+                        table[slab * halves + h, 16 * i : 16 * i + 16, at] = high
+                        table[slab * halves + h, GRID + 16 * i : GRID + 16 * i + 16, at] = rest
+            return inner
+
+        lax.fori_loop(0, halves, block_tables, 0)
+        return carry
+
+    lax.fori_loop(0, ranks, slab_tables, 0)
+    sent_share(True)
+
+    def spread_half(slab, h):
+        highs, lows = [], []
+        for j in range(4):
+            b = 4 * h + j
+            y, dy = yq[slab * blocks + b, 0], yq[slab * blocks + b, 1]
+            none = jnp.zeros((kys, TILE), F32)
+            lead, tail = [none] * 8, [none] * 8
+            for k in range(ORDER):
+                lead[j + k] = vx[k, pl.ds(b, 1), :] * y + vx[ORDER + k, pl.ds(b, 1), :] * dy
+                tail[j + k] = vx[2 * ORDER + k, pl.ds(b, 1), :] * y
+            both = jnp.concatenate(
+                [jnp.concatenate(lead, axis=0), jnp.concatenate(tail, axis=0)], axis=1
+            )
+            high, rest = split(both)
+            highs.append(high)
+            lows.append(rest)
+        left = jnp.concatenate(
+            [jnp.concatenate(highs, axis=1), jnp.concatenate(lows, axis=1)], axis=0
+        )
+        sums = lax.dot_general(
+            left, table[slab * halves + h], CONTRACT_LANES, preferred_element_type=F32
+        )
+        count = 8 * kys
+        at = pl.ds(pl.multiple_of((slab * planes + 4 * h) * kys, 4 * kys), count)
+        grid[at, :] += sums[:count, :GRID] + sums[:count, GRID:] + sums[count:, :GRID]
+
+    def gather_half(slab, h):
+        count = 8 * kys
+        at = pl.ds(pl.multiple_of((slab * planes + 4 * h) * kys, 4 * kys), count)
+        sums = dot(jnp.concatenate([wide[at, :], low[at, :]], axis=0), table[slab * halves + h])
+        for j in range(4):
+            b = 4 * h + j
+            one = two = three = 0.0
+            for k in range(ORDER):
+                rows = slice((j + k) * kys, (j + k + 1) * kys)
+                more = slice(count + (j + k) * kys, count + (j + k + 1) * kys)
+                value, slope = slice(2 * j * TILE, (2 * j + 1) * TILE), slice((2 * j + 1) * TILE, (2 * j + 2) * TILE)
+                plain = sums[rows, value] + sums[more, value]
+                tilted = sums[rows, slope] + sums[more, slope]
+                x, dx = xw[slab, k, pl.ds(b, 1), :], xw[slab, ORDER + k, pl.ds(b, 1), :]
+                one += dx * plain
+                two += x * plain
+                three += x * tilted
+            y, dy = yq[slab * blocks + b, 0], yq[slab * blocks + b, 1]
+            for c, term in enumerate((y * one, dy * two, y * three)):
+                out_part[slab, c, pl.ds(b, 1), :] = jnp.sum(term, axis=0, keepdims=True)
+
+    def sweep(it, carry):
+        @pl.when(it > 0)
+        def _():
+            start_share(False)
+            got_share(1, False)
+            got_share(2, False)
+
+        for e in range(blocks + 2 * HALO_BLK):
+            slab = lax.rem(me + (ranks - 1 if e < HALO_BLK else 0 if e < HALO_BLK + blocks else 1), ranks)
+            row = (e - HALO_BLK) % blocks
+            spread_columns(e, [info[slab, FIELD0 + c, row : row + 1, :] for c in range(3)])
+
+        def one_home(b, inner):
+            def one_source(k, sums):
+                sums = list(sums)
+                for j in range(TILE // 8):
+                    rows = slice(8 * j, 8 * j + 8)
+                    v = [cols[b + k, c, rows, :] for c in range(3)]
+                    w = [tens[b * reach + k, 1 + c, rows, :] for c in range(3)]
+                    third = tens[b * reach + k, 0, rows, :]
+                    along = w[0] * v[0] + w[1] * v[1] + w[2] * v[2]
+                    for c in range(3):
+                        sums[c] = sums[c] + third * v[c]
+                        sums[3 + c] = sums[3 + c] + along * w[c]
+                return tuple(sums)
+
+            sums = lax.fori_loop(0, reach, one_source, (jnp.zeros((8, TILE), F32),) * 6)
+            for c in range(3):
+                pair[c, pl.ds(b, 1), :] = jnp.sum(sums[c] - sums[3 + c], axis=0, keepdims=True)
+            return inner
+
+        lax.fori_loop(0, blocks, one_home, 0)
+
+        grid[...] = jnp.zeros_like(grid)
+
+        def spread_slab(d, inner):
+            @pl.when((it > 0) & (d > 2))
+            def _():
+                got_share(d, False)
+
+            slab = lax.rem(me + away(d), ranks)
+            v = [info[slab, FIELD0 + c] for c in range(3)]
+            for k in range(ORDER):
+                x, dx = xw[slab, k], xw[slab, ORDER + k]
+                vx[k] = v[0] * dx
+                vx[ORDER + k] = v[1] * x
+                vx[2 * ORDER + k] = v[2] * x
+            for h in range(halves):
+                spread_half(slab, h)
+            return inner
+
+        lax.fori_loop(0, ranks, spread_slab, 0)
+
+        size = GRID * kys
+        edge = 2 * kys
+        grid[size : size + edge, :] += grid[0:edge, :]
+        grid[edge : 2 * edge, :] += grid[size + edge : size + 2 * edge, :]
+
+        step = 2 * GRID
+        for i in range(size // step):
+            high, rest = split(grid[edge + i * step : edge + (i + 1) * step, :])
+            sums = dot(jnp.concatenate([high, rest], axis=1), zin_ref[...])
+            spec[i * step : (i + 1) * step, :] = sums[:, :GRID] + sums[:, GRID:]
+        for q in range(0, kys, 2):
+            pairs = [pl.ds(q, GRID, stride=kys), pl.ds(q + 1, GRID, stride=kys)]
+            high, rest = split(jnp.concatenate([spec[s, :] for s in pairs], axis=1))
+            line = dot(xin_ref[...], jnp.concatenate([high, rest, high], axis=0))
+            line = line * jnp.concatenate([green[q], green[q + 1]], axis=1)
+            high, rest = split(line)
+            line = dot(xout_ref[...], jnp.concatenate([high, rest, high], axis=0))
+            spec[pairs[0], :] = line[:, :GRID]
+            spec[pairs[1], :] = line[:, GRID:]
+        for i in range(size // step):
+            high, rest = split(spec[i * step : (i + 1) * step, :])
+            sums = dot(jnp.concatenate([high, rest], axis=1), zout_ref[...])
+            high, rest = split(sums[:, :GRID] + sums[:, GRID:])
+            rows = slice(edge + i * step, edge + (i + 1) * step)
+            wide[rows, :] = jnp.concatenate([high, high], axis=1)
+            low[rows, :] = jnp.concatenate([rest, jnp.zeros_like(rest)], axis=1)
+        for ref in (wide, low):
+            ref[0:edge, :] = ref[size : size + edge, :]
+            ref[size + edge : size + 2 * edge, :] = ref[edge : 2 * edge, :]
+
+        def gather_slab(t, inner):
+            off = away(ranks - 1 - t)
+            slab = lax.rem(me + off, ranks)
+            for h in range(halves):
+                gather_half(slab, h)
+
+            @pl.when(t < ranks - 1)
+            def _():
+                fold(off, slab).start()
+
+            return inner
+
+        lax.fori_loop(0, ranks, gather_slab, 0)
+
+        @pl.when(it > 0)
+        def _():
+            sent_share(False)
+
+        def landed(i, inner):
+            fold(i, lax.rem(me + i, ranks)).wait()
+            return inner
+
+        lax.fori_loop(1, ranks, landed, 0)
+        for c in range(3):
+            total = out_part[me, c]
+            for i in range(1, ranks):
+                total = total + in_part[i, c]
+            following = pair[c] - total
+            bases[it + 1, c] = following
+            info[me, FIELD0 + c] = following / polar_ref[...]
+        return carry
+
+    lax.fori_loop(0, ITERS, sweep, 0)
+
+    count = ITERS + 1
+    place_of = {}
+    part[...] = jnp.zeros_like(part)
+    for i in range(count):
+        for j in range(i, count):
+            place_of[i, j] = place_of[j, i] = row = len(set(place_of.values()))
+            value = 0.0
+            for c in range(3):
+                value += bases[i, c] * (bases[j, c] / polar_ref[...])
+            part[row : row + 1, :] = jnp.sum(value, axis=0, keepdims=True)
+
+    def tell(i, row):
+        return pltpu.make_async_remote_copy(
+            src_ref=part, dst_ref=slots.at[lax.rem(me + row, ranks)], send_sem=gram_send.at[i], recv_sem=gram_recv.at[i],
+            device_id={"gx": lax.rem(me + i, ranks)}, device_id_type=pl.DeviceIdType.MESH,
+        )
+
+    def tell_start(i, carry):
+        tell(i, 0).start()
+        return carry
+
+    def tell_wait(i, carry):
+        tell(i, ranks - i).wait()
+        return carry
+
+    lax.fori_loop(1, ranks, tell_start, 0)
+    slots[me] = part[...]
+    lax.fori_loop(1, ranks, tell_wait, 0)
+    sums = jnp.sum(jnp.sum(slots[...], axis=0), axis=1, keepdims=True)
+    sums = jnp.broadcast_to(sums, (sums.shape[0], TILE))
+    dipoles, residual = krylov(sums, place_of, count)
+    for c in range(3):
+        basis = [bases[i, c] for i in range(count)]
+        first = combine(dipoles, [b / polar_ref[...] for b in basis])
+        second = combine(residual, basis)
+        for b in range(blocks):
+            dip_ref[c : c + 1, lanes(b)] = first[b : b + 1, :]
+            res_ref[c : c + 1, lanes(b)] = second[b : b + 1, :]
+
+
+def krylov(sums, place, count):
+    def inner(x, y):
+        value = None
+        for i in range(count):
+            for j in range(count):
+                if x[i] is not None and y[j] is not None:
+                    row = place[i, j]
+                    term = x[i] * y[j] * sums[row : row + 1]
+                    value = term if value is None else value + term
+        return value
+
+    none = [None] * (count - 1)
+    residual = [jnp.ones((1, TILE), F32)] + none
+    direction = list(residual)
+    dipoles = [None] * count
+    rz_now = inner(residual, residual)
+    for sweep in range(ITERS):
+        image = scaled(-1.0, direction, [None] + direction[:-1])
+        step = rz_now / inner(direction, image)
+        dipoles = scaled(step, dipoles, direction)
+        residual = scaled(-step, residual, image)
+        if sweep + 1 < ITERS:
+            rz_next = inner(residual, residual)
+            direction = scaled(rz_next / rz_now, residual, direction)
+            rz_now = rz_next
+    return dipoles, residual
+
+
+def fast_shapes(ranks, blocks):
+    kys = GRID // ranks
+    ext_blocks = blocks + 2 * HALO_BLK
+    rows = (GRID + 4) * kys
+    dma = pltpu.SemaphoreType.DMA
+    tile = (blocks, TILE)
+    buffers = [
+        ((2, blocks * TILE, GRID), F32),
+        ((ranks, 8) + tile, F32),
+        ((ranks * blocks // 4, 2 * GRID, 8 * TILE), BF16),
+        ((ranks * blocks, 2, kys, TILE), F32),
+        ((ranks, 2 * ORDER) + tile, F32),
+        ((2, 2 * ORDER) + tile, F32),
+        ((3 * ORDER,) + tile, F32),
+        ((rows, GRID), F32),
+        ((GRID * kys, GRID), F32),
+        ((rows, 2 * GRID), BF16),
+        ((rows, 2 * GRID), BF16),
+        ((kys, GRID, GRID), F32),
+        ((blocks * (2 * HALO_BLK + 1), 4, TILE, TILE), F32),
+        ((ext_blocks, 3, TILE, TILE), F32),
+        ((3,) + tile, F32),
+        ((2, 3) + tile, F32),
+        ((ext_blocks, 8, TILE), F32),
+        ((ITERS + 1, 3) + tile, F32),
+        ((3,) + tile, F32),
+        ((ranks, 3) + tile, F32),
+        ((ranks, 3) + tile, F32),
+        ((16, TILE), F32),
+        ((ranks, 16, TILE), F32),
+    ]
+    sems = [dma((2,))] + [dma((ranks,))] * 4 + [dma((2,))] * 2 + [dma((ranks,))] * 2
+    return buffers, sems
+
+
+def fits_fast(ranks, blocks):
+    if blocks != 8 or GRID % ranks or GRID // ranks != blocks:
+        return False
+    buffers, _ = fast_shapes(ranks, blocks)
+    return sum(int(np.prod(s)) * np.dtype(t).itemsize for s, t in buffers) < 50 * 1024 * 1024
+
+
+def halves_of(x):
+    high = x.astype(BF16)
+    return high, (x - high.astype(np.float32)).astype(BF16)
+
+
+def fast_device(positions, field, inv_polar, x_spline, yz_spline, tile_list, tile_count):
+    ranks = lax.axis_size("gx")
+    atoms_here = positions.shape[1]
+    blocks = atoms_here // TILE
+    line = np.arange(GRID)
+    center = (line[None, :] - line[:, None] + GRID // 2) % GRID - GRID // 2
+    center = np.concatenate([center, np.eye(GRID)], axis=0)
+    center = np.concatenate([center.astype(np.float32).astype(BF16)] * 3, axis=1)
+    rows = fixed_rows(line)
+
+    def along_z(m):
+        high, rest = halves_of(np.ascontiguousarray(m))
+        return np.concatenate(
+            [np.concatenate([high, rest], axis=1), np.concatenate([high, np.zeros_like(rest)], axis=1)], axis=0
+        )
+
+    def along_x(m):
+        high, rest = halves_of(np.ascontiguousarray(m))
+        return np.concatenate([high, high, rest], axis=1)
+
+    constants = [center, along_z(rows.T), along_z(rows), along_x(rows), along_x(rows.T)]
+    buffers, sems = fast_shapes(ranks, blocks)
+    smem = pl.BlockSpec(memory_space=pltpu.SMEM)
+    return pl.pallas_call(
+        functools.partial(fast_kernel, ranks),
+        in_specs=[VMEM] * 4 + [smem] * 2 + [VMEM] * 5 + [pl.BlockSpec(memory_space=pl.ANY)],
+        out_specs=[VMEM] * 2,
+        out_shape=[jax.ShapeDtypeStruct(positions.shape, F32)] * 2,
+        scratch_shapes=[pltpu.VMEM(s, t) for s, t in buffers] + sems,
+        compiler_params=pltpu.CompilerParams(
+            vmem_limit_bytes=62 * 1024 * 1024, collective_id=2, has_side_effects=True
+        ),
+        name="induced",
+    )(
+        positions, field, inv_polar.reshape(blocks, TILE), x_spline.transpose(1, 0, 2),
+        tile_list, tile_count, *[jnp.asarray(c) for c in constants], yz_spline,
+    )
+
+
 def solution(mesh):
     placed = (
         P(None, ("rep", "gx")),
@@ -521,8 +1115,14 @@
         P(("rep", "gx"), None),
         P(("rep", "gx")),
     )
+    ranks = mesh.shape["gx"]
+
+    def choose(*arrays):
+        device = fast_device if fits_fast(ranks, arrays[0].shape[1] // TILE) else per_device
+        return device(*arrays)
+
     return jax.shard_map(
-        per_device,
+        choose,
         mesh=mesh,
         in_specs=placed,
         out_specs=(P(None, ("rep", "gx")), P(None, ("rep", "gx"))),

time: 195 us -> 116 us (0.59)
  Pallas kernels: 183 us -> 112 us
  other arithmetic: 4.07 us -> 0 us
  local copies, waits for them, and re-layouts: 5.59 us -> 2.65 us
    pallas_call x11 -> x1, Pallas kernels: 183 us -> 112 us  [fast_device(): pl.pallas_call(functools.partial(fast_kernel, ranks), in_specs=[VMEM] * 4...]
    unnamed x4 -> x2, local copies, waits for them, and re-layouts: 4.21 us -> 2.65 us
where the time goes in v1:
time: 116 us; the launch traced here: 115 us
  Pallas kernels  112 us (97%)
  local copies, waits for them, and re-layouts  2.65 us (2%)
    pallas_call x1, Pallas kernels, fast_device(): pl.pallas_call(functools.partial(fast_kernel, ranks), in_specs=[VMEM] * 4...  112 us
    unnamed x2, local copies, waits for them, and re-layouts  2.65 us

profile of v1, /device:TPU:0, one launch (start us, length us, event | category | flops | bytes accessed | tf_op | source)
XLA Modules:
  0.0 115.2 jit_solution(14926111322391900637)
XLA Ops:
  0.6 112.0 %induced.1 = (f32[3,1024]{1,0:T(4,128)}, f32[3,1024]{1,0:T(4,128)}) custom-call(f32[3,1024]{1,0:T(4,128)} %pos_ref.1, f32[3,1024]{1,0:T(4,128)} %field_ref.1, f32[8,128]{1,0:T(8,128)} %bitcast.3, f32[5,2,1024]{2,1,0:T(2,128)} %bitcast.2, s32[8,7]{1,0:T(8,128)} %list_ref.1, s32[8]{0:T(128)} %count_ref.1, bf16[256,384]{1,0:T(8,128)(2,1)} %constant.10.clone.center_ref, ...), custom_call_target="tpu_custom_call" | custom-call | tf_op jit(solution)/shard_map/induced/pallas_call | solution.py:1092
  112.6 1.3 %copy.16 = f32[3,1024]{1,0:T(4,128)} copy(f32[3,1024]{1,0:T(4,128)} %get-tuple-element.4) | data formatting | bytes 24576
  113.9 1.3 %copy.17 = f32[3,1024]{1,0:T(4,128)} copy(f32[3,1024]{1,0:T(4,128)} %get-tuple-element.5) | data formatting | bytes 24576

commit v2 on v1

--- a/solution.py
+++ b/solution.py
@@ -544,6 +544,14 @@
     return 1.0 - 2.0 * sine * sine, 2.0 * sine * cosine
 
 
+def total_of(x):
+    return jnp.sum(jnp.sum(x, axis=0, keepdims=True), axis=1, keepdims=True)
+
+
+def pick(rows, index):
+    return jnp.take_along_axis(rows, index, axis=0, mode="promise_in_bounds")
+
+
 def iota(shape, dim):
     return lax.broadcasted_iota(jnp.int32, shape, dim)
 
@@ -553,10 +561,10 @@
 
 def fast_kernel(
     ranks, pos_ref, field_ref, polar_ref, xs_ref, list_ref, count_ref,
-    center_ref, zin_ref, zout_ref, xin_ref, xout_ref, yz_ref,
+    center_ref, eye_ref, zin_ref, zout_ref, xin_ref, xout_ref, yz_ref,
     dip_ref, res_ref,
-    lines, info, table, yq, xw, wt, vx, grid, spec, wide, low, green, tens, cols, place, sides, ext,
-    bases, pair, out_part, in_part, part, slots,
+    lines, info, table, flipped, yq, xw, wt, wz, vx, mix, hold, grid, spec, wide, low, green, tens, cols, place, sides, ext,
+    bases, pair, out_part, in_part, part, slots, energy,
     local_sem, ag_send, ag_recv, rs_send, rs_recv, side_send, side_recv, gram_send, gram_recv,
 ):
     me = lax.axis_index("gx")
@@ -588,6 +596,19 @@
     for c in range(3):
         for b in range(blocks):
             place[c, b : b + 1, :] = pos_ref[c : c + 1, lanes(b)]
+    with jax.named_scope("greet_wait"):
+        pl.semaphore_wait(barrier, ranks - 1)
+    neighbours = [
+        pltpu.make_async_remote_copy(
+            src_ref=place, dst_ref=sides.at[t], send_sem=side_send.at[t], recv_sem=side_recv.at[t],
+            device_id={"gx": lax.rem(me + step, ranks)}, device_id_type=pl.DeviceIdType.MESH,
+        )
+        for t, step in enumerate((1, ranks - 1))
+    ]
+    for copy in neighbours:
+        copy.start()
+    for c in range(3):
+        for b in range(blocks):
             bases[0, c, b : b + 1, :] = field_ref[c : c + 1, lanes(b)]
     for c in range(3):
         info[me, FIELD0 + c] = bases[0, c] / polar_ref[...]
@@ -596,29 +617,29 @@
         offset = offset + (1.0 * k) * xs_ref[k, 0:1, :]
     for b in range(blocks):
         info[me, 4, b : b + 1, :] = offset[:, lanes(b)]
-    for load in loads:
-        load.wait()
+    with jax.named_scope("yz_wait"):
+        for load in loads:
+            load.wait()
     marks = iota((GRID, TILE), 0).astype(F32)
-    for t in range(2):
-        for b in range(blocks):
-            line = lines[t, lanes(b), :]
-            high = line.astype(BF16)
-            rest = line - high.astype(F32)
-            mid, tail = split(rest)
-            moment = lax.dot_general(
-                center_ref[...], jnp.concatenate([high, mid, tail], axis=1), CONTRACT_LANES,
-                preferred_element_type=F32,
-            )
-            moment, weight = moment[:GRID], moment[GRID:]
-            best = jnp.max(
-                jnp.where((jnp.abs(moment) < 0.5001) & (weight > 0.25), marks, -1.0), axis=0, keepdims=True
-            )
-            shift = jnp.sum(jnp.where(marks == best, moment, 0.0), axis=0, keepdims=True)
-            start = best - 2.0
-            info[me, 2 * t, b : b + 1, :] = jnp.where(start < 0, start + GRID, start)
-            info[me, 2 * t + 1, b : b + 1, :] = shift + 0.5
-
-    pl.semaphore_wait(barrier, ranks - 1)
+    with jax.named_scope("moments"):
+        for t in range(2):
+            for b in range(blocks):
+                line = lines[t, lanes(b), :]
+                high = line.astype(BF16)
+                rest = line - high.astype(F32)
+                mid, tail = split(rest)
+                moment = lax.dot_general(
+                    center_ref[...], jnp.concatenate([high, mid, tail], axis=1), CONTRACT_LANES,
+                    preferred_element_type=F32,
+                )
+                moment, weight = moment[:GRID], moment[GRID:]
+                best = jnp.max(
+                    jnp.where((jnp.abs(moment) < 0.5001) & (weight > 0.25), marks, -1.0), axis=0, keepdims=True
+                )
+                shift = jnp.sum(jnp.where(marks == best, moment, 0.0), axis=0, keepdims=True)
+                start = best - 2.0
+                info[me, 2 * t, b : b + 1, :] = jnp.where(start < 0, start + GRID, start)
+                info[me, 2 * t + 1, b : b + 1, :] = shift + 0.5
 
     def share(i, first, source=None):
         owner = me if source is None else source
@@ -657,16 +678,6 @@
         share(lax.rem(ranks - off, ranks), first, lax.rem(me + off, ranks)).wait_recv()
 
     start_share(True)
-    neighbours = [
-        pltpu.make_async_remote_copy(
-            src_ref=place, dst_ref=sides.at[t], send_sem=side_send.at[t], recv_sem=side_recv.at[t],
-            device_id={"gx": lax.rem(me + step, ranks)}, device_id_type=pl.DeviceIdType.MESH,
-        )
-        for t, step in enumerate((1, ranks - 1))
-    ]
-    for copy in neighbours:
-        copy.start()
-
     def modes(freq):
         number = jnp.where(freq <= GRID // 2, freq, freq - GRID // 2)
         return number.astype(F32), jnp.where((freq == 0) | (freq == GRID // 2), 1.0 / GRID, 2.0 / GRID)
@@ -684,10 +695,12 @@
         green[q] = value * (flat_weights * y_weights)
         return carry
 
-    lax.fori_loop(0, kys, filter_one, 0)
-
-    for copy in neighbours:
-        copy.wait()
+    with jax.named_scope("filter"):
+        lax.fori_loop(0, kys, filter_one, 0)
+
+    with jax.named_scope("side_wait"):
+        for copy in neighbours:
+            copy.wait()
 
     def spread_columns(e, rows):
         for c in range(3):
@@ -709,7 +722,8 @@
         spread_columns(e, [ext[e, c : c + 1, :] for c in range(3)])
         return carry
 
-    lax.fori_loop(0, blocks + 2 * HALO_BLK, position_columns, 0)
+    with jax.named_scope("poscols"):
+        lax.fori_loop(0, blocks + 2 * HALO_BLK, position_columns, 0)
     lag = iota((8, TILE), 1) - iota((8, TILE), 0)
 
     def tensors(index, carry):
@@ -726,12 +740,13 @@
             live = jnp.where(lag != 8 * j + hide, near, 0.0)
             square = live * inverse * inverse
             tens[index, 0, rows, :] = PAIR_C * (square * inverse)
-            weight = (3.0 * PAIR_C) ** 0.5 * (square * jnp.sqrt(inverse))
+            weight = (3.0 * PAIR_C) ** 0.5 * (square * inverse * lax.rsqrt(inverse))
             for c in range(3):
                 tens[index, 1 + c, rows, :] = weight * r[c]
         return carry
 
-    lax.fori_loop(0, blocks * reach, tensors, 0)
+    with jax.named_scope("tensors"):
+        lax.fori_loop(0, blocks * reach, tensors, 0)
 
     freq = me * kys + iota((kys, TILE), 0)
     sine_mode = freq > GRID // 2
@@ -739,10 +754,42 @@
     lead_in = jnp.where(sine_mode, GRID // 4, 0).astype(F32)
     shifts = [turn(number * (1.0 * k)) for k in range(ORDER)]
 
+    wz[...] = jnp.zeros_like(wz)
+
+    def flip(at):
+        for j in range(4):
+            both = slice(2 * j * TILE, (2 * j + 2) * TILE)
+            turned = lax.dot_general(
+                eye_ref[...], table[at, :, both], CONTRACT_LANES, preferred_element_type=F32
+            )
+            flipped[at, both, :] = turned.astype(BF16)
+
+    def block_tables(slab, b):
+        at, j = slab * halves + b // 4, b % 4
+        first = jnp.broadcast_to(info[slab, 0, b : b + 1, :], (kys, TILE))
+        cosine, sine = turn(number * first - lead_in)
+        for t in range(2):
+            rows = [wt[ORDER * t + k, b : b + 1, :] for k in range(ORDER)]
+            real = combine([s[0] for s in shifts], rows)
+            imag = combine([s[1] for s in shifts], rows)
+            yq[slab * blocks + b, t] = cosine * real - sine * imag
+        begin = jnp.broadcast_to(info[slab, 2, b : b + 1, :], (8, TILE)).astype(jnp.int32)
+        for i in range(GRID // 16):
+            gaps = [
+                jnp.minimum((iota((8, TILE), 0) + (16 * i + 8 * r - begin)) & (GRID - 1), 7)
+                for r in range(2)
+            ]
+            for t in range(2):
+                dense = jnp.concatenate([pick(wz[t, b], gap) for gap in gaps], axis=0)
+                high, rest = split(dense)
+                table[at, 16 * i : 16 * i + 16, lanes(2 * j + t)] = high
+                table[at, GRID + 16 * i : GRID + 16 * i + 16, lanes(2 * j + t)] = rest
+
     def slab_tables(d, carry):
-        @pl.when(d > 0)
-        def _():
-            got_share(d, True)
+        with jax.named_scope("info_wait"):
+            @pl.when(d > 0)
+            def _():
+                got_share(d, True)
 
         slab = lax.rem(me + away(d), ranks)
         values, slopes = spline_rows(info[slab, 4])
@@ -752,99 +799,215 @@
         for t in range(2):
             values, slopes = spline_rows(info[slab, 2 * t + 1])
             for k in range(ORDER):
-                wt[t, k] = values[k]
-                wt[t, ORDER + k] = slopes[k]
-
-        def block_tables(h, inner):
+                if t == 0:
+                    wt[k] = values[k]
+                    wt[ORDER + k] = slopes[k]
+                else:
+                    for b in range(blocks):
+                        wz[0, b, k : k + 1, :] = values[k][b : b + 1, :]
+                        wz[1, b, k : k + 1, :] = slopes[k][b : b + 1, :]
+
+        before = lax.rem(me + away(jnp.maximum(d - 1, 0)), ranks) * halves + halves - 1
+        with jax.named_scope("tables"):
+            for h in range(halves):
+                flip(before if h == 0 else slab * halves + h - 1)
+                for j in range(4):
+                    block_tables(slab, 4 * h + j)
+        return carry
+
+    lax.fori_loop(0, ranks, slab_tables, 0)
+    flip(lax.rem(me + away(ranks - 1), ranks) * halves + halves - 1)
+    sent_share(True)
+
+    def weigh(slab, slot):
+        v = [info[slab, FIELD0 + c] for c in range(3)]
+        for k in range(ORDER):
+            x, dx = xw[slab, k], xw[slab, ORDER + k]
+            vx[slot, k] = v[0] * dx
+            vx[slot, ORDER + k] = v[1] * x
+            vx[slot, 2 * ORDER + k] = v[2] * x
+        for h in range(halves):
             for j in range(4):
                 b = 4 * h + j
-
-                def row(t, k):
-                    return wt[t, k, pl.ds(b, 1), :]
-
-                first = jnp.broadcast_to(info[slab, 0, pl.ds(b, 1), :], (kys, TILE))
-                cosine, sine = turn(number * first - lead_in)
-                for t in range(2):
-                    real = combine([s[0] for s in shifts], [row(0, ORDER * t + k) for k in range(ORDER)])
-                    imag = combine([s[1] for s in shifts], [row(0, ORDER * t + k) for k in range(ORDER)])
-                    yq[slab * blocks + b, t] = cosine * real - sine * imag
-                begin = info[slab, 2, pl.ds(b, 1), :].astype(jnp.int32)
-                for i in range(GRID // 16):
-                    gap = (iota((16, TILE), 0) + (16 * i - begin)) & (GRID - 1)
-                    for t in range(2):
-                        dense = jnp.zeros((16, TILE), F32)
-                        for k in range(ORDER):
-                            dense = jnp.where(gap == k, row(1, ORDER * t + k), dense)
-                        high, rest = split(dense)
-                        at = slice((2 * j + t) * TILE, (2 * j + t + 1) * TILE)
-                        table[slab * halves + h, 16 * i : 16 * i + 16, at] = high
-                        table[slab * halves + h, GRID + 16 * i : GRID + 16 * i + 16, at] = rest
+                y, dy = yq[slab * blocks + b, 0], yq[slab * blocks + b, 1]
+                none = jnp.zeros((kys, TILE), F32)
+                lead, tail = [none] * 8, [none] * 8
+                for k in range(ORDER):
+                    lead[j + k] = vx[slot, k, b : b + 1, :] * y + vx[slot, ORDER + k, b : b + 1, :] * dy
+                    tail[j + k] = vx[slot, 2 * ORDER + k, b : b + 1, :] * y
+                for t, pieces in enumerate((lead, tail)):
+                    high, rest = split(jnp.concatenate(pieces, axis=0))
+                    mix[slot, h, : 8 * kys, lanes(2 * j + t)] = high
+                    mix[slot, h, 8 * kys :, lanes(2 * j + t)] = rest
+
+    def window(slab, h):
+        return pl.ds(pl.multiple_of((slab * planes + 4 * h) * kys, 4 * kys), 8 * kys)
+
+    def spread_slab(slab, slot):
+        count = 8 * kys
+        for h in range(halves):
+            sums = dot(mix[slot, h], flipped[slab * halves + h])
+            grid[window(slab, h), :] += sums[:count, :GRID] + sums[:count, GRID:] + sums[count:, :GRID]
+
+    def read_slab(slab, slot):
+        for h in range(halves):
+            at = window(slab, h)
+            left = jnp.concatenate([wide[at, :], low[at, :]], axis=0)
+            hold[slot, h] = dot(left, table[slab * halves + h])
+
+    def gather_slab(slab, slot):
+        count = 8 * kys
+        for h in range(halves):
+            for j in range(4):
+                b = 4 * h + j
+                one = two = three = 0.0
+                for k in range(ORDER):
+                    rows = slice((j + k) * kys, (j + k + 1) * kys)
+                    more = slice(count + (j + k) * kys, count + (j + k + 1) * kys)
+                    plain = hold[slot, h, rows, lanes(2 * j)] + hold[slot, h, more, lanes(2 * j)]
+                    tilted = hold[slot, h, rows, lanes(2 * j + 1)] + hold[slot, h, more, lanes(2 * j + 1)]
+                    x, dx = xw[slab, k, b : b + 1, :], xw[slab, ORDER + k, b : b + 1, :]
+                    one += dx * plain
+                    two += x * plain
+                    three += x * tilted
+                y, dy = yq[slab * blocks + b, 0], yq[slab * blocks + b, 1]
+                for c, term in enumerate((y * one, dy * two, y * three)):
+                    out_part[slab, c, b : b + 1, :] = jnp.sum(term, axis=0, keepdims=True)
+
+    count = ITERS + 1
+    entries = {}
+    for i in range(ITERS):
+        for j in range(i, ITERS):
+            entries[i, j] = entries[j, i] = len(set(entries.values()))
+    last = len(set(entries.values()))
+    for i in range(ITERS - 1):
+        entries[i, ITERS] = entries[i + 1, ITERS - 1]
+    entries[ITERS - 1, ITERS] = last
+
+    def tell(i, row):
+        return pltpu.make_async_remote_copy(
+            src_ref=part, dst_ref=slots.at[lax.rem(me + row, ranks)], send_sem=gram_send.at[i],
+            recv_sem=gram_recv.at[i], device_id={"gx": lax.rem(me + i, ranks)},
+            device_id_type=pl.DeviceIdType.MESH,
+        )
+
+    def send_products():
+        column = iota((1, TILE), 1)
+        packed = jnp.zeros((1, TILE), F32)
+        for i in range(ITERS):
+            for j in range(i, ITERS):
+                value = 0.0
+                for c in range(3):
+                    value += bases[i, c] * (bases[j, c] / polar_ref[...])
+                packed = jnp.where(column == entries[i, j], total_of(value), packed)
+        value = 0.0
+        for c in range(3):
+            value += pair[c] * info[me, FIELD0 + c]
+        packed = jnp.where(column == last, total_of(value) - total_of(energy[...]), packed)
+        part[...] = packed
+        slots[me] = packed
+
+        def one(i, carry):
+            tell(i, 0).start()
+            return carry
+
+        lax.fori_loop(1, ranks, one, 0)
+
+    def sweep(it, carry):
+        with jax.named_scope("near_wait"):
+            @pl.when(it > 0)
+            def _():
+                start_share(False)
+
+        grid[...] = jnp.zeros_like(grid)
+
+        def slab_at(d):
+            return lax.rem(me + away(jnp.minimum(d, ranks - 1)), ranks)
+
+        def vector_columns(n):
+            n = jnp.minimum(n, blocks + 2 * HALO_BLK - 1)
+            e = jnp.where(n < blocks, n + HALO_BLK, jnp.where(n < blocks + HALO_BLK, n - blocks, n))
+            step = jnp.where(e < HALO_BLK, ranks - 1, jnp.where(e < HALO_BLK + blocks, 0, 1))
+            slab = lax.rem(me + step, ranks)
+            row = lax.rem(e + blocks - HALO_BLK, blocks)
+            spread_columns(e, [info[slab, FIELD0 + c, pl.ds(row, 1), :] for c in range(3)])
+
+        def spread_two(m, inner):
+            with jax.named_scope("far_wait"):
+                for d in (2 * m + 1, 2 * m + 2):
+
+                    @pl.when((it > 0) & (d < ranks))
+                    def _(d=d):
+                        got_share(d, False)
+
+            with jax.named_scope("spread"):
+                weigh(slab_at(2 * m + 1), 1)
+                spread_slab(slab_at(2 * m), 0)
+                for n in (2 * m, 2 * m + 1):
+                    vector_columns(n)
+                weigh(slab_at(2 * m + 2), 0)
+                spread_slab(slab_at(2 * m + 1), 1)
             return inner
 
-        lax.fori_loop(0, halves, block_tables, 0)
-        return carry
-
-    lax.fori_loop(0, ranks, slab_tables, 0)
-    sent_share(True)
-
-    def spread_half(slab, h):
-        highs, lows = [], []
-        for j in range(4):
-            b = 4 * h + j
-            y, dy = yq[slab * blocks + b, 0], yq[slab * blocks + b, 1]
-            none = jnp.zeros((kys, TILE), F32)
-            lead, tail = [none] * 8, [none] * 8
-            for k in range(ORDER):
-                lead[j + k] = vx[k, pl.ds(b, 1), :] * y + vx[ORDER + k, pl.ds(b, 1), :] * dy
-                tail[j + k] = vx[2 * ORDER + k, pl.ds(b, 1), :] * y
-            both = jnp.concatenate(
-                [jnp.concatenate(lead, axis=0), jnp.concatenate(tail, axis=0)], axis=1
-            )
-            high, rest = split(both)
-            highs.append(high)
-            lows.append(rest)
-        left = jnp.concatenate(
-            [jnp.concatenate(highs, axis=1), jnp.concatenate(lows, axis=1)], axis=0
-        )
-        sums = lax.dot_general(
-            left, table[slab * halves + h], CONTRACT_LANES, preferred_element_type=F32
-        )
-        count = 8 * kys
-        at = pl.ds(pl.multiple_of((slab * planes + 4 * h) * kys, 4 * kys), count)
-        grid[at, :] += sums[:count, :GRID] + sums[:count, GRID:] + sums[count:, :GRID]
-
-    def gather_half(slab, h):
-        count = 8 * kys
-        at = pl.ds(pl.multiple_of((slab * planes + 4 * h) * kys, 4 * kys), count)
-        sums = dot(jnp.concatenate([wide[at, :], low[at, :]], axis=0), table[slab * halves + h])
-        for j in range(4):
-            b = 4 * h + j
-            one = two = three = 0.0
-            for k in range(ORDER):
-                rows = slice((j + k) * kys, (j + k + 1) * kys)
-                more = slice(count + (j + k) * kys, count + (j + k + 1) * kys)
-                value, slope = slice(2 * j * TILE, (2 * j + 1) * TILE), slice((2 * j + 1) * TILE, (2 * j + 2) * TILE)
-                plain = sums[rows, value] + sums[more, value]
-                tilted = sums[rows, slope] + sums[more, slope]
-                x, dx = xw[slab, k, pl.ds(b, 1), :], xw[slab, ORDER + k, pl.ds(b, 1), :]
-                one += dx * plain
-                two += x * plain
-                three += x * tilted
-            y, dy = yq[slab * blocks + b, 0], yq[slab * blocks + b, 1]
-            for c, term in enumerate((y * one, dy * two, y * three)):
-                out_part[slab, c, pl.ds(b, 1), :] = jnp.sum(term, axis=0, keepdims=True)
-
-    def sweep(it, carry):
-        @pl.when(it > 0)
-        def _():
-            start_share(False)
-            got_share(1, False)
-            got_share(2, False)
-
-        for e in range(blocks + 2 * HALO_BLK):
-            slab = lax.rem(me + (ranks - 1 if e < HALO_BLK else 0 if e < HALO_BLK + blocks else 1), ranks)
-            row = (e - HALO_BLK) % blocks
-            spread_columns(e, [info[slab, FIELD0 + c, row : row + 1, :] for c in range(3)])
+        weigh(me, 0)
+        lax.fori_loop(0, ranks // 2, spread_two, 0)
+
+        with jax.named_scope("fold"):
+            size = GRID * kys
+            edge = 2 * kys
+            grid[size : size + edge, :] += grid[0:edge, :]
+            grid[edge : 2 * edge, :] += grid[size + edge : size + 2 * edge, :]
+
+        step = 2 * GRID
+        with jax.named_scope("zin"):
+            for i in range(size // step):
+                high, rest = split(grid[edge + i * step : edge + (i + 1) * step, :])
+                sums = dot(jnp.concatenate([high, rest], axis=1), zin_ref[...])
+                spec[i * step : (i + 1) * step, :] = sums[:, :GRID] + sums[:, GRID:]
+        with jax.named_scope("xinout"):
+            power = jnp.zeros((8, GRID), F32)
+            for q in range(0, kys, 2):
+                pairs = [pl.ds(q, GRID, stride=kys), pl.ds(q + 1, GRID, stride=kys)]
+                high, rest = split(jnp.concatenate([spec[s, :] for s in pairs], axis=1))
+                line = dot(xin_ref[...], jnp.concatenate([high, rest, high], axis=0))
+                passed = line * jnp.concatenate([green[q], green[q + 1]], axis=1)
+                worth = line * passed
+                power += jnp.sum((worth[:, :GRID] + worth[:, GRID:]).reshape(GRID // 8, 8, GRID), axis=0)
+                line = passed
+                high, rest = split(line)
+                line = dot(xout_ref[...], jnp.concatenate([high, rest, high], axis=0))
+                spec[pairs[0], :] = line[:, :GRID]
+                spec[pairs[1], :] = line[:, GRID:]
+            energy[...] = power
+        with jax.named_scope("zout"):
+            for i in range(size // step):
+                high, rest = split(spec[i * step : (i + 1) * step, :])
+                sums = dot(jnp.concatenate([high, rest], axis=1), zout_ref[...])
+                high, rest = split(sums[:, :GRID] + sums[:, GRID:])
+                rows = slice(edge + i * step, edge + (i + 1) * step)
+                wide[rows, :] = jnp.concatenate([high, high], axis=1)
+                low[rows, :] = jnp.concatenate([rest, jnp.zeros_like(rest)], axis=1)
+            for ref in (wide, low):
+                ref[0:edge, :] = ref[size : size + edge, :]
+                ref[size + edge : size + 2 * edge, :] = ref[edge : 2 * edge, :]
+
+        def gather_two(m, inner):
+            first, second = ranks - 1 - 2 * m, ranks - 2 - 2 * m
+            with jax.named_scope("gather"):
+                read_slab(slab_at(second), 1)
+                gather_slab(slab_at(first), 0)
+                read_slab(slab_at(jnp.maximum(second - 1, 0)), 0)
+                gather_slab(slab_at(second), 1)
+            fold(away(first), slab_at(first)).start()
+
+            @pl.when(second > 0)
+            def _():
+                fold(away(second), slab_at(second)).start()
+
+            return inner
+
+        read_slab(slab_at(ranks - 1), 0)
+        lax.fori_loop(0, ranks // 2, gather_two, 0)
 
         def one_home(b, inner):
             def one_source(k, sums):
@@ -865,123 +1028,46 @@
                 pair[c, pl.ds(b, 1), :] = jnp.sum(sums[c] - sums[3 + c], axis=0, keepdims=True)
             return inner
 
-        lax.fori_loop(0, blocks, one_home, 0)
-
-        grid[...] = jnp.zeros_like(grid)
-
-        def spread_slab(d, inner):
-            @pl.when((it > 0) & (d > 2))
+        with jax.named_scope("pair"):
+            lax.fori_loop(0, blocks, one_home, 0)
+
+        @pl.when(it == ITERS - 1)
+        def _():
+            with jax.named_scope("gram"):
+                send_products()
+
+        with jax.named_scope("sent_wait"):
+            @pl.when(it > 0)
             def _():
-                got_share(d, False)
-
-            slab = lax.rem(me + away(d), ranks)
-            v = [info[slab, FIELD0 + c] for c in range(3)]
-            for k in range(ORDER):
-                x, dx = xw[slab, k], xw[slab, ORDER + k]
-                vx[k] = v[0] * dx
-                vx[ORDER + k] = v[1] * x
-                vx[2 * ORDER + k] = v[2] * x
-            for h in range(halves):
-                spread_half(slab, h)
-            return inner
-
-        lax.fori_loop(0, ranks, spread_slab, 0)
-
-        size = GRID * kys
-        edge = 2 * kys
-        grid[size : size + edge, :] += grid[0:edge, :]
-        grid[edge : 2 * edge, :] += grid[size + edge : size + 2 * edge, :]
-
-        step = 2 * GRID
-        for i in range(size // step):
-            high, rest = split(grid[edge + i * step : edge + (i + 1) * step, :])
-            sums = dot(jnp.concatenate([high, rest], axis=1), zin_ref[...])
-            spec[i * step : (i + 1) * step, :] = sums[:, :GRID] + sums[:, GRID:]
-        for q in range(0, kys, 2):
-            pairs = [pl.ds(q, GRID, stride=kys), pl.ds(q + 1, GRID, stride=kys)]
-            high, rest = split(jnp.concatenate([spec[s, :] for s in pairs], axis=1))
-            line = dot(xin_ref[...], jnp.concatenate([high, rest, high], axis=0))
-            line = line * jnp.concatenate([green[q], green[q + 1]], axis=1)
-            high, rest = split(line)
-            line = dot(xout_ref[...], jnp.concatenate([high, rest, high], axis=0))
-            spec[pairs[0], :] = line[:, :GRID]
-            spec[pairs[1], :] = line[:, GRID:]
-        for i in range(size // step):
-            high, rest = split(spec[i * step : (i + 1) * step, :])
-            sums = dot(jnp.concatenate([high, rest], axis=1), zout_ref[...])
-            high, rest = split(sums[:, :GRID] + sums[:, GRID:])
-            rows = slice(edge + i * step, edge + (i + 1) * step)
-            wide[rows, :] = jnp.concatenate([high, high], axis=1)
-            low[rows, :] = jnp.concatenate([rest, jnp.zeros_like(rest)], axis=1)
-        for ref in (wide, low):
-            ref[0:edge, :] = ref[size : size + edge, :]
-            ref[size + edge : size + 2 * edge, :] = ref[edge : 2 * edge, :]
-
-        def gather_slab(t, inner):
-            off = away(ranks - 1 - t)
-            slab = lax.rem(me + off, ranks)
-            for h in range(halves):
-                gather_half(slab, h)
-
-            @pl.when(t < ranks - 1)
-            def _():
-                fold(off, slab).start()
-
-            return inner
-
-        lax.fori_loop(0, ranks, gather_slab, 0)
-
-        @pl.when(it > 0)
-        def _():
-            sent_share(False)
+                sent_share(False)
 
         def landed(i, inner):
             fold(i, lax.rem(me + i, ranks)).wait()
             return inner
 
-        lax.fori_loop(1, ranks, landed, 0)
-        for c in range(3):
-            total = out_part[me, c]
-            for i in range(1, ranks):
-                total = total + in_part[i, c]
-            following = pair[c] - total
-            bases[it + 1, c] = following
-            info[me, FIELD0 + c] = following / polar_ref[...]
+        with jax.named_scope("rs_wait"):
+            lax.fori_loop(1, ranks, landed, 0)
+        with jax.named_scope("update"):
+            for c in range(3):
+                total = out_part[me, c]
+                for i in range(1, ranks):
+                    total = total + in_part[i, c]
+                following = pair[c] - total
+                bases[it + 1, c] = following
+                info[me, FIELD0 + c] = following / polar_ref[...]
         return carry
 
     lax.fori_loop(0, ITERS, sweep, 0)
-
-    count = ITERS + 1
-    place_of = {}
-    part[...] = jnp.zeros_like(part)
-    for i in range(count):
-        for j in range(i, count):
-            place_of[i, j] = place_of[j, i] = row = len(set(place_of.values()))
-            value = 0.0
-            for c in range(3):
-                value += bases[i, c] * (bases[j, c] / polar_ref[...])
-            part[row : row + 1, :] = jnp.sum(value, axis=0, keepdims=True)
-
-    def tell(i, row):
-        return pltpu.make_async_remote_copy(
-            src_ref=part, dst_ref=slots.at[lax.rem(me + row, ranks)], send_sem=gram_send.at[i], recv_sem=gram_recv.at[i],
-            device_id={"gx": lax.rem(me + i, ranks)}, device_id_type=pl.DeviceIdType.MESH,
-        )
-
-    def tell_start(i, carry):
-        tell(i, 0).start()
-        return carry
 
     def tell_wait(i, carry):
         tell(i, ranks - i).wait()
         return carry
 
-    lax.fori_loop(1, ranks, tell_start, 0)
-    slots[me] = part[...]
-    lax.fori_loop(1, ranks, tell_wait, 0)
-    sums = jnp.sum(jnp.sum(slots[...], axis=0), axis=1, keepdims=True)
-    sums = jnp.broadcast_to(sums, (sums.shape[0], TILE))
-    dipoles, residual = krylov(sums, place_of, count)
+    with jax.named_scope("gram_wait"):
+        lax.fori_loop(1, ranks, tell_wait, 0)
+    sums = jnp.sum(slots[...], axis=0)
+    sums = {r: jnp.broadcast_to(sums[:, r : r + 1], (1, TILE)) for r in range(last + 1)}
+    dipoles, residual = krylov(sums, entries, count)
     for c in range(3):
         basis = [bases[i, c] for i in range(count)]
         first = combine(dipoles, [b / polar_ref[...] for b in basis])
@@ -998,7 +1084,7 @@
             for j in range(count):
                 if x[i] is not None and y[j] is not None:
                     row = place[i, j]
-                    term = x[i] * y[j] * sums[row : row + 1]
+                    term = x[i] * y[j] * sums[row]
                     value = term if value is None else value + term
         return value
 
@@ -1029,10 +1115,14 @@
         ((2, blocks * TILE, GRID), F32),
         ((ranks, 8) + tile, F32),
         ((ranks * blocks // 4, 2 * GRID, 8 * TILE), BF16),
+        ((ranks * blocks // 4, 8 * TILE, 2 * GRID), BF16),
         ((ranks * blocks, 2, kys, TILE), F32),
         ((ranks, 2 * ORDER) + tile, F32),
-        ((2, 2 * ORDER) + tile, F32),
-        ((3 * ORDER,) + tile, F32),
+        ((2 * ORDER,) + tile, F32),
+        ((2, blocks, 8, TILE), F32),
+        ((2, 3 * ORDER) + tile, F32),
+        ((2, blocks // 4, 16 * kys, 8 * TILE), BF16),
+        ((2, blocks // 4, 16 * kys, 8 * TILE), F32),
         ((rows, GRID), F32),
         ((GRID * kys, GRID), F32),
         ((rows, 2 * GRID), BF16),
@@ -1047,8 +1137,9 @@
         ((3,) + tile, F32),
         ((ranks, 3) + tile, F32),
         ((ranks, 3) + tile, F32),
-        ((16, TILE), F32),
-        ((ranks, 16, TILE), F32),
+        ((1, TILE), F32),
+        ((ranks, 1, TILE), F32),
+        ((8, GRID), F32),
     ]
     sems = [dma((2,))] + [dma((ranks,))] * 4 + [dma((2,))] * 2 + [dma((ranks,))] * 2
     return buffers, sems
@@ -1058,7 +1149,7 @@
     if blocks != 8 or GRID % ranks or GRID // ranks != blocks:
         return False
     buffers, _ = fast_shapes(ranks, blocks)
-    return sum(int(np.prod(s)) * np.dtype(t).itemsize for s, t in buffers) < 50 * 1024 * 1024
+    return sum(int(np.prod(s)) * np.dtype(t).itemsize for s, t in buffers) < 60 * 1024 * 1024
 
 
 def halves_of(x):
@@ -1086,12 +1177,13 @@
         high, rest = halves_of(np.ascontiguousarray(m))
         return np.concatenate([high, high, rest], axis=1)
 
-    constants = [center, along_z(rows.T), along_z(rows), along_x(rows), along_x(rows.T)]
+    eye = np.eye(2 * TILE, dtype=np.float32).astype(BF16)
+    constants = [center, eye, along_z(rows.T), along_z(rows), along_x(rows), along_x(rows.T)]
     buffers, sems = fast_shapes(ranks, blocks)
     smem = pl.BlockSpec(memory_space=pltpu.SMEM)
     return pl.pallas_call(
         functools.partial(fast_kernel, ranks),
-        in_specs=[VMEM] * 4 + [smem] * 2 + [VMEM] * 5 + [pl.BlockSpec(memory_space=pl.ANY)],
+        in_specs=[VMEM] * 4 + [smem] * 2 + [VMEM] * len(constants) + [pl.BlockSpec(memory_space=pl.ANY)],
         out_specs=[VMEM] * 2,
         out_shape=[jax.ShapeDtypeStruct(positions.shape, F32)] * 2,
         scratch_shapes=[pltpu.VMEM(s, t) for s, t in buffers] + sems,

time: 116 us -> 91.1 us (0.79)
  Pallas kernels: 112 us -> 87.4 us
    pallas_call x1, Pallas kernels: 112 us -> 87.4 us  [fast_device(): pl.pallas_call(functools.partial(fast_kernel, ranks), in_specs=[VMEM] * 4...]
where the time goes in v2:
time: 91.1 us; the launch traced here: 90.7 us
  Pallas kernels  87.4 us (96%)
  local copies, waits for them, and re-layouts  2.65 us (3%)
    pallas_call x1, Pallas kernels, fast_device(): pl.pallas_call(functools.partial(fast_kernel, ranks), in_specs=[VMEM] * 4...  87.4 us
    unnamed x2, local copies, waits for them, and re-layouts  2.65 us

profile of v2, /device:TPU:0, one launch (start us, length us, event | category | flops | bytes accessed | tf_op | source)
XLA Modules:
  0.0 90.7 jit_solution(11024977925254409681)
XLA Ops:
  0.6 87.4 %induced.1 = (f32[3,1024]{1,0:T(4,128)}, f32[3,1024]{1,0:T(4,128)}) custom-call(f32[3,1024]{1,0:T(4,128)} %pos_ref.1, f32[3,1024]{1,0:T(4,128)} %field_ref.1, f32[8,128]{1,0:T(8,128)} %bitcast.3, f32[5,2,1024]{2,1,0:T(2,128)} %bitcast.2, s32[8,7]{1,0:T(8,128)} %list_ref.1, s32[8]{0:T(128)} %count_ref.1, bf16[256,384]{1,0:T(8,128)(2,1)} %constant.12.clone.center_ref, ...), custom_call_target="tpu_custom_call" | custom-call | tf_op jit(solution)/shard_map/induced/pallas_call | solution.py:1184
  88.1 1.3 %copy.17 = f32[3,1024]{1,0:T(4,128)} copy(f32[3,1024]{1,0:T(4,128)} %get-tuple-element.4) | data formatting | bytes 24576
  89.4 1.3 %copy.18 = f32[3,1024]{1,0:T(4,128)} copy(f32[3,1024]{1,0:T(4,128)} %get-tuple-element.5) | data formatting | bytes 24576

commit v3 on v2

--- a/solution.py
+++ b/solution.py
@@ -564,8 +564,9 @@
     center_ref, eye_ref, zin_ref, zout_ref, xin_ref, xout_ref, yz_ref,
     dip_ref, res_ref,
     lines, info, table, flipped, yq, xw, wt, wz, vx, mix, hold, grid, spec, wide, low, green, tens, cols, place, sides, ext,
-    bases, pair, out_part, in_part, part, slots, energy,
-    local_sem, ag_send, ag_recv, rs_send, rs_recv, side_send, side_recv, gram_send, gram_recv,
+    bases, pair, out_part, pair_part, in_part, part, slots, energy,
+    local_sem, all_send, all_recv, gram_send, gram_recv, side_send, side_recv,
+    ag_send, ag_recv, on_send, on_recv, pair_send, pair_recv, rs_send, rs_recv,
 ):
     me = lax.axis_index("gx")
     blocks = polar_ref.shape[0]
@@ -596,17 +597,6 @@
     for c in range(3):
         for b in range(blocks):
             place[c, b : b + 1, :] = pos_ref[c : c + 1, lanes(b)]
-    with jax.named_scope("greet_wait"):
-        pl.semaphore_wait(barrier, ranks - 1)
-    neighbours = [
-        pltpu.make_async_remote_copy(
-            src_ref=place, dst_ref=sides.at[t], send_sem=side_send.at[t], recv_sem=side_recv.at[t],
-            device_id={"gx": lax.rem(me + step, ranks)}, device_id_type=pl.DeviceIdType.MESH,
-        )
-        for t, step in enumerate((1, ranks - 1))
-    ]
-    for copy in neighbours:
-        copy.start()
     for c in range(3):
         for b in range(blocks):
             bases[0, c, b : b + 1, :] = field_ref[c : c + 1, lanes(b)]
@@ -641,43 +631,99 @@
                 info[me, 2 * t, b : b + 1, :] = jnp.where(start < 0, start + GRID, start)
                 info[me, 2 * t + 1, b : b + 1, :] = shift + 0.5
 
-    def share(i, first, source=None):
-        owner = me if source is None else source
-        span = info.at[owner] if first else info.at[owner, pl.ds(FIELD0, 3)]
+    with jax.named_scope("greet_wait"):
+        pl.semaphore_wait(barrier, ranks - 1)
+    neighbours = [
+        pltpu.make_async_remote_copy(
+            src_ref=place, dst_ref=sides.at[t], send_sem=side_send.at[t], recv_sem=side_recv.at[t],
+            device_id={"gx": lax.rem(me + step, ranks)}, device_id_type=pl.DeviceIdType.MESH,
+        )
+        for t, step in enumerate((1, ranks - 1))
+    ]
+    for copy in neighbours:
+        copy.start()
+
+    mesh_id = pl.DeviceIdType.MESH
+    chips = ranks // 2
+    rows_of_chips = chips // 2
+    core, chip = lax.rem(me, 2), me // 2
+    partner = me + 1 - 2 * core
+
+    def away(d, count):
+        step = (d + 1) // 2
+        return lax.rem(jnp.where(d % 2 == 1, step, count - step), count)
+
+    def slab_at(d):
+        return lax.rem(me + away(d, ranks), ranks)
+
+    def tell_all(i, owner):
         return pltpu.make_async_remote_copy(
-            src_ref=span, dst_ref=span, send_sem=ag_send.at[i], recv_sem=ag_recv.at[i],
-            device_id={"gx": lax.rem(me + i, ranks)}, device_id_type=pl.DeviceIdType.MESH,
-        )
-
-    def fold(i, slab):
+            src_ref=info.at[owner], dst_ref=info.at[owner], send_sem=all_send.at[i], recv_sem=all_recv.at[i],
+            device_id={"gx": lax.rem(me + i, ranks)}, device_id_type=mesh_id,
+        )
+
+    def got_all(d):
+        off = away(d, ranks)
+        tell_all(lax.rem(ranks - off, ranks), lax.rem(me + off, ranks)).wait_recv()
+
+    def chip_at(d):
+        down, side = away(d // 2, rows_of_chips), d % 2
+        return lax.rem(chip // 2 + down, rows_of_chips) * 2 + lax.rem(chip % 2 + side, 2)
+
+    def mirrored(d):
+        down, side = away(d // 2, rows_of_chips), d % 2
+        return lax.rem(rows_of_chips - down, rows_of_chips) * 2 + side
+
+    def forth(d):
+        return away(d // 2, rows_of_chips) * 2 + d % 2
+
+    def same(d):
+        return 2 * chip_at(d) + core
+
+    def other(d):
+        return 2 * chip_at(d) + 1 - core
+
+    def vector(owner):
+        return info.at[owner, pl.ds(FIELD0, 3)]
+
+    def direct(d):
         return pltpu.make_async_remote_copy(
-            src_ref=out_part.at[slab], dst_ref=in_part.at[i], send_sem=rs_send.at[i], recv_sem=rs_recv.at[i],
-            device_id={"gx": slab}, device_id_type=pl.DeviceIdType.MESH,
-        )
-
-    def away(d):
-        step = (d + 1) // 2
-        return lax.rem(jnp.where(d % 2 == 1, step, ranks - step), ranks)
-
-    def start_share(first):
+            src_ref=vector(me), dst_ref=vector(me), send_sem=ag_send.at[forth(d)], recv_sem=ag_recv.at[forth(d)],
+            device_id={"gx": same(d)}, device_id_type=mesh_id,
+        )
+
+    def got_direct(d):
+        pltpu.make_async_remote_copy(
+            src_ref=vector(same(d)), dst_ref=vector(same(d)), send_sem=ag_send.at[mirrored(d)],
+            recv_sem=ag_recv.at[mirrored(d)], device_id={"gx": same(d)}, device_id_type=mesh_id,
+        ).wait_recv()
+
+    def forward(d, owner):
+        return pltpu.make_async_remote_copy(
+            src_ref=vector(owner), dst_ref=vector(owner), send_sem=on_send.at[d], recv_sem=on_recv.at[d],
+            device_id={"gx": partner}, device_id_type=mesh_id,
+        )
+
+    def hand_over(d):
+        return pltpu.make_async_remote_copy(
+            src_ref=out_part.at[other(d)], dst_ref=pair_part.at[d], send_sem=pair_send.at[d],
+            recv_sem=pair_recv.at[d], device_id={"gx": partner}, device_id_type=mesh_id,
+        )
+
+    def fold(d):
+        return pltpu.make_async_remote_copy(
+            src_ref=out_part.at[same(d)], dst_ref=in_part.at[forth(d)], send_sem=rs_send.at[forth(d)],
+            recv_sem=rs_recv.at[forth(d)], device_id={"gx": same(d)}, device_id_type=mesh_id,
+        )
+
+    def each(low, high, act):
         def one(d, carry):
-            share(away(d), first).start()
+            act(d)
             return carry
 
-        lax.fori_loop(1, ranks, one, 0)
-
-    def sent_share(first):
-        def one(i, carry):
-            share(i, first).wait_send()
-            return carry
-
-        lax.fori_loop(1, ranks, one, 0)
-
-    def got_share(d, first):
-        off = away(d)
-        share(lax.rem(ranks - off, ranks), first, lax.rem(me + off, ranks)).wait_recv()
-
-    start_share(True)
+        lax.fori_loop(low, high, one, 0)
+
+    each(1, ranks, lambda d: tell_all(away(d, ranks), me).start())
     def modes(freq):
         number = jnp.where(freq <= GRID // 2, freq, freq - GRID // 2)
         return number.astype(F32), jnp.where((freq == 0) | (freq == GRID // 2), 1.0 / GRID, 2.0 / GRID)
@@ -698,32 +744,31 @@
     with jax.named_scope("filter"):
         lax.fori_loop(0, kys, filter_one, 0)
 
+    def spread_columns(e, rows):
+        for c in range(3):
+            cols[e, c] = jnp.broadcast_to(rows[c], (TILE, TILE)).T
+
+    def position_columns(e, carry):
+        spread_columns(e, [ext[e, c : c + 1, :] for c in range(3)])
+        return carry
+
+    for e in range(blocks):
+        for c in range(3):
+            ext[e + HALO_BLK, c : c + 1, :] = place[c, e : e + 1, :]
+    with jax.named_scope("poscols"):
+        lax.fori_loop(HALO_BLK, HALO_BLK + blocks, position_columns, 0)
     with jax.named_scope("side_wait"):
         for copy in neighbours:
             copy.wait()
-
-    def spread_columns(e, rows):
+    for e in range(HALO_BLK):
         for c in range(3):
-            cols[e, c] = jnp.broadcast_to(rows[c], (TILE, TILE)).T
-
-    for e in range(blocks + 2 * HALO_BLK):
-        for c in range(3):
-            if e < HALO_BLK:
-                row = blocks - HALO_BLK + e
-                value = sides[0, c, row : row + 1, :] - (1.0 * blocks if c == 0 else 0.0)
-            elif e < HALO_BLK + blocks:
-                value = place[c, e - HALO_BLK : e - HALO_BLK + 1, :]
-            else:
-                row = e - HALO_BLK - blocks
-                value = sides[1, c, row : row + 1, :] + (1.0 * blocks if c == 0 else 0.0)
-            ext[e, c : c + 1, :] = value
-
-    def position_columns(e, carry):
-        spread_columns(e, [ext[e, c : c + 1, :] for c in range(3)])
-        return carry
-
-    with jax.named_scope("poscols"):
-        lax.fori_loop(0, blocks + 2 * HALO_BLK, position_columns, 0)
+            move = 1.0 * blocks if c == 0 else 0.0
+            row = blocks - HALO_BLK + e
+            ext[e, c : c + 1, :] = sides[0, c, row : row + 1, :] - move
+            ext[blocks + HALO_BLK + e, c : c + 1, :] = sides[1, c, e : e + 1, :] + move
+    with jax.named_scope("poscols2"):
+        lax.fori_loop(0, HALO_BLK, position_columns, 0)
+        lax.fori_loop(HALO_BLK + blocks, 2 * HALO_BLK + blocks, position_columns, 0)
     lag = iota((8, TILE), 1) - iota((8, TILE), 0)
 
     def tensors(index, carry):
@@ -756,11 +801,15 @@
 
     wz[...] = jnp.zeros_like(wz)
 
+    def beside(ref, at, parts):
+        return jnp.concatenate([ref[at, t] for t in parts], axis=1)
+
     def flip(at):
         for j in range(4):
             both = slice(2 * j * TILE, (2 * j + 2) * TILE)
             turned = lax.dot_general(
-                eye_ref[...], table[at, :, both], CONTRACT_LANES, preferred_element_type=F32
+                eye_ref[...], beside(table, at, range(2 * j, 2 * j + 2)), CONTRACT_LANES,
+                preferred_element_type=F32,
             )
             flipped[at, both, :] = turned.astype(BF16)
 
@@ -782,16 +831,16 @@
             for t in range(2):
                 dense = jnp.concatenate([pick(wz[t, b], gap) for gap in gaps], axis=0)
                 high, rest = split(dense)
-                table[at, 16 * i : 16 * i + 16, lanes(2 * j + t)] = high
-                table[at, GRID + 16 * i : GRID + 16 * i + 16, lanes(2 * j + t)] = rest
+                table[at, 2 * j + t, 16 * i : 16 * i + 16, :] = high
+                table[at, 2 * j + t, GRID + 16 * i : GRID + 16 * i + 16, :] = rest
 
     def slab_tables(d, carry):
         with jax.named_scope("info_wait"):
             @pl.when(d > 0)
             def _():
-                got_share(d, True)
-
-        slab = lax.rem(me + away(d), ranks)
+                got_all(d)
+
+        slab = slab_at(d)
         values, slopes = spline_rows(info[slab, 4])
         for k in range(ORDER):
             xw[slab, k] = values[k]
@@ -807,7 +856,7 @@
                         wz[0, b, k : k + 1, :] = values[k][b : b + 1, :]
                         wz[1, b, k : k + 1, :] = slopes[k][b : b + 1, :]
 
-        before = lax.rem(me + away(jnp.maximum(d - 1, 0)), ranks) * halves + halves - 1
+        before = slab_at(jnp.maximum(d - 1, 0)) * halves + halves - 1
         with jax.named_scope("tables"):
             for h in range(halves):
                 flip(before if h == 0 else slab * halves + h - 1)
@@ -816,8 +865,8 @@
         return carry
 
     lax.fori_loop(0, ranks, slab_tables, 0)
-    flip(lax.rem(me + away(ranks - 1), ranks) * halves + halves - 1)
-    sent_share(True)
+    flip(slab_at(ranks - 1) * halves + halves - 1)
+    each(1, ranks, lambda i: tell_all(i, me).wait_send())
 
     def weigh(slab, slot):
         v = [info[slab, FIELD0 + c] for c in range(3)]
@@ -852,8 +901,12 @@
     def read_slab(slab, slot):
         for h in range(halves):
             at = window(slab, h)
-            left = jnp.concatenate([wide[at, :], low[at, :]], axis=0)
-            hold[slot, h] = dot(left, table[slab * halves + h])
+            high, rest = wide[at, :], low[at, :]
+            left = jnp.concatenate(
+                [jnp.concatenate([high, rest], axis=0), jnp.concatenate([high, jnp.zeros_like(rest)], axis=0)],
+                axis=1,
+            )
+            hold[slot, h] = dot(left, beside(table, slab * halves + h, range(8)))
 
     def gather_slab(slab, slot):
         count = 8 * kys
@@ -913,44 +966,104 @@
 
         lax.fori_loop(1, ranks, one, 0)
 
+    def vector_columns(n):
+        n = jnp.minimum(n, blocks + 2 * HALO_BLK - 1)
+        e = jnp.where(n < blocks, n + HALO_BLK, jnp.where(n < blocks + HALO_BLK, n - blocks, n))
+        step = jnp.where(e < HALO_BLK, ranks - 1, jnp.where(e < HALO_BLK + blocks, 0, 1))
+        slab = lax.rem(me + step, ranks)
+        row = lax.rem(e + blocks - HALO_BLK, blocks)
+        spread_columns(e, [info[slab, FIELD0 + c, pl.ds(row, 1), :] for c in range(3)])
+
+    def pair_rows(b, low, high, fresh):
+        def one_source(k, sums):
+            sums = list(sums)
+            for j in range(TILE // 8):
+                rows = slice(8 * j, 8 * j + 8)
+                v = [cols[b + k, c, rows, :] for c in range(3)]
+                w = [tens[b * reach + k, 1 + c, rows, :] for c in range(3)]
+                third = tens[b * reach + k, 0, rows, :]
+                along = w[0] * v[0] + w[1] * v[1] + w[2] * v[2]
+                for c in range(3):
+                    sums[c] = sums[c] + third * v[c]
+                    sums[3 + c] = sums[3 + c] + along * w[c]
+            return tuple(sums)
+
+        sums = lax.fori_loop(low, high, one_source, (jnp.zeros((8, TILE), F32),) * 6)
+        for c in range(3):
+            value = jnp.sum(sums[c] - sums[3 + c], axis=0, keepdims=True)
+            if fresh:
+                pair[c, pl.ds(b, 1), :] = value
+            else:
+                pair[c, pl.ds(b, 1), :] += value
+
+    def pair_own():
+        each(0, blocks, lambda b: pair_rows(
+            b, jnp.maximum(HALO_BLK - b, 0), jnp.minimum(blocks + HALO_BLK - b, reach), True
+        ))
+
+    def pair_edges():
+        each(0, HALO_BLK, lambda b: pair_rows(b, 0, HALO_BLK - b, False))
+        each(blocks - HALO_BLK, blocks, lambda b: pair_rows(b, blocks + HALO_BLK - b, reach, False))
+
     def sweep(it, carry):
+        @pl.when(it > 0)
+        def _():
+            forward(0, me).start()
+            each(1, chips, lambda d: direct(d).start())
+
+        grid[...] = jnp.zeros_like(grid)
+
+        def pass_on(d):
+            got_direct(d)
+            forward(d, same(d)).start()
+
+        def spread_two(m, inner):
+            following = jnp.minimum(m + 1, chips - 1)
+            with jax.named_scope("far_wait"):
+
+                @pl.when((it > 0) & (m + 2 < chips))
+                def _():
+                    pass_on(m + 2)
+
+                @pl.when(it > 0)
+                def _():
+                    forward(m, other(m)).wait_recv()
+
+            with jax.named_scope("spread"):
+                weigh(other(m), 1)
+                spread_slab(same(m), 0)
+                first = jnp.where(m < blocks // 2, 2 * m, jnp.maximum(2 * m - 2, blocks - 2))
+                for n in (first, first + 1):
+                    vector_columns(n)
+                weigh(same(following), 0)
+                spread_slab(other(m), 1)
+            return inner
+
+        weigh(me, 0)
+
+        @pl.when(it == ITERS - 1)
+        def _():
+            with jax.named_scope("pair"):
+                each(0, blocks, vector_columns)
+                pair_own()
+
         with jax.named_scope("near_wait"):
+
             @pl.when(it > 0)
             def _():
-                start_share(False)
-
-        grid[...] = jnp.zeros_like(grid)
-
-        def slab_at(d):
-            return lax.rem(me + away(jnp.minimum(d, ranks - 1)), ranks)
-
-        def vector_columns(n):
-            n = jnp.minimum(n, blocks + 2 * HALO_BLK - 1)
-            e = jnp.where(n < blocks, n + HALO_BLK, jnp.where(n < blocks + HALO_BLK, n - blocks, n))
-            step = jnp.where(e < HALO_BLK, ranks - 1, jnp.where(e < HALO_BLK + blocks, 0, 1))
-            slab = lax.rem(me + step, ranks)
-            row = lax.rem(e + blocks - HALO_BLK, blocks)
-            spread_columns(e, [info[slab, FIELD0 + c, pl.ds(row, 1), :] for c in range(3)])
-
-        def spread_two(m, inner):
-            with jax.named_scope("far_wait"):
-                for d in (2 * m + 1, 2 * m + 2):
-
-                    @pl.when((it > 0) & (d < ranks))
-                    def _(d=d):
-                        got_share(d, False)
-
-            with jax.named_scope("spread"):
-                weigh(slab_at(2 * m + 1), 1)
-                spread_slab(slab_at(2 * m), 0)
-                for n in (2 * m, 2 * m + 1):
-                    vector_columns(n)
-                weigh(slab_at(2 * m + 2), 0)
-                spread_slab(slab_at(2 * m + 1), 1)
-            return inner
-
-        weigh(me, 0)
-        lax.fori_loop(0, ranks // 2, spread_two, 0)
+                pass_on(1)
+
+        lax.fori_loop(0, chips, spread_two, 0)
+
+        @pl.when(it > 0)
+        def _():
+            forward(0, me).wait_send()
+            each(1, chips, lambda d: forward(d, same(d)).wait_send())
+
+        @pl.when(it == ITERS - 1)
+        def _():
+            with jax.named_scope("pair"):
+                pair_edges()
 
         with jax.named_scope("fold"):
             size = GRID * kys
@@ -979,78 +1092,72 @@
                 spec[pairs[0], :] = line[:, :GRID]
                 spec[pairs[1], :] = line[:, GRID:]
             energy[...] = power
+
+        @pl.when(it == ITERS - 1)
+        def _():
+            with jax.named_scope("gram"):
+                send_products()
         with jax.named_scope("zout"):
             for i in range(size // step):
                 high, rest = split(spec[i * step : (i + 1) * step, :])
                 sums = dot(jnp.concatenate([high, rest], axis=1), zout_ref[...])
                 high, rest = split(sums[:, :GRID] + sums[:, GRID:])
                 rows = slice(edge + i * step, edge + (i + 1) * step)
-                wide[rows, :] = jnp.concatenate([high, high], axis=1)
-                low[rows, :] = jnp.concatenate([rest, jnp.zeros_like(rest)], axis=1)
+                wide[rows, :] = high
+                low[rows, :] = rest
             for ref in (wide, low):
                 ref[0:edge, :] = ref[size : size + edge, :]
                 ref[size + edge : size + 2 * edge, :] = ref[edge : 2 * edge, :]
 
+        def turn_of(t):
+            d = chips - 1 - lax.rem(t, chips)
+            return 2 * chip_at(d) + jnp.where(t < chips, 1 - core, core)
+
         def gather_two(m, inner):
-            first, second = ranks - 1 - 2 * m, ranks - 2 - 2 * m
             with jax.named_scope("gather"):
-                read_slab(slab_at(second), 1)
-                gather_slab(slab_at(first), 0)
-                read_slab(slab_at(jnp.maximum(second - 1, 0)), 0)
-                gather_slab(slab_at(second), 1)
-            fold(away(first), slab_at(first)).start()
-
-            @pl.when(second > 0)
-            def _():
-                fold(away(second), slab_at(second)).start()
+                read_slab(turn_of(2 * m + 1), 1)
+                gather_slab(turn_of(2 * m), 0)
+                read_slab(turn_of(jnp.minimum(2 * m + 2, ranks - 1)), 0)
+                gather_slab(turn_of(2 * m + 1), 1)
+            for t in (2 * m, 2 * m + 1):
+                d = chips - 1 - lax.rem(t, chips)
+
+                @pl.when(t < chips)
+                def _(d=d):
+                    hand_over(d).start()
+
+                @pl.when(t >= chips)
+                def _(d=d):
+                    hand_over(d).wait_recv()
+                    for c in range(3):
+                        out_part[same(d), c] += pair_part[d, c]
+
+                @pl.when((t >= chips) & (d > 0))
+                def _(d=d):
+                    fold(d).start()
 
             return inner
 
-        read_slab(slab_at(ranks - 1), 0)
-        lax.fori_loop(0, ranks // 2, gather_two, 0)
-
-        def one_home(b, inner):
-            def one_source(k, sums):
-                sums = list(sums)
-                for j in range(TILE // 8):
-                    rows = slice(8 * j, 8 * j + 8)
-                    v = [cols[b + k, c, rows, :] for c in range(3)]
-                    w = [tens[b * reach + k, 1 + c, rows, :] for c in range(3)]
-                    third = tens[b * reach + k, 0, rows, :]
-                    along = w[0] * v[0] + w[1] * v[1] + w[2] * v[2]
-                    for c in range(3):
-                        sums[c] = sums[c] + third * v[c]
-                        sums[3 + c] = sums[3 + c] + along * w[c]
-                return tuple(sums)
-
-            sums = lax.fori_loop(0, reach, one_source, (jnp.zeros((8, TILE), F32),) * 6)
-            for c in range(3):
-                pair[c, pl.ds(b, 1), :] = jnp.sum(sums[c] - sums[3 + c], axis=0, keepdims=True)
-            return inner
-
-        with jax.named_scope("pair"):
-            lax.fori_loop(0, blocks, one_home, 0)
-
-        @pl.when(it == ITERS - 1)
+        read_slab(turn_of(0), 0)
+        lax.fori_loop(0, chips, gather_two, 0)
+
+        @pl.when(it < ITERS - 1)
         def _():
-            with jax.named_scope("gram"):
-                send_products()
-
-        with jax.named_scope("sent_wait"):
-            @pl.when(it > 0)
-            def _():
-                sent_share(False)
-
-        def landed(i, inner):
-            fold(i, lax.rem(me + i, ranks)).wait()
-            return inner
-
+            with jax.named_scope("pair"):
+                pair_own()
+                pair_edges()
+
+        @pl.when(it > 0)
+        def _():
+            each(1, chips, lambda d: direct(d).wait_send())
+
+        each(0, chips, lambda d: hand_over(d).wait_send())
         with jax.named_scope("rs_wait"):
-            lax.fori_loop(1, ranks, landed, 0)
+            each(1, chips, lambda d: fold(d).wait())
         with jax.named_scope("update"):
             for c in range(3):
                 total = out_part[me, c]
-                for i in range(1, ranks):
+                for i in range(1, chips):
                     total = total + in_part[i, c]
                 following = pair[c] - total
                 bases[it + 1, c] = following
@@ -1114,7 +1221,7 @@
     buffers = [
         ((2, blocks * TILE, GRID), F32),
         ((ranks, 8) + tile, F32),
-        ((ranks * blocks // 4, 2 * GRID, 8 * TILE), BF16),
+        ((ranks * blocks // 4, 8, 2 * GRID, TILE), BF16),
         ((ranks * blocks // 4, 8 * TILE, 2 * GRID), BF16),
         ((ranks * blocks, 2, kys, TILE), F32),
         ((ranks, 2 * ORDER) + tile, F32),
@@ -1125,8 +1232,8 @@
         ((2, blocks // 4, 16 * kys, 8 * TILE), F32),
         ((rows, GRID), F32),
         ((GRID * kys, GRID), F32),
-        ((rows, 2 * GRID), BF16),
-        ((rows, 2 * GRID), BF16),
+        ((rows, GRID), BF16),
+        ((rows, GRID), BF16),
         ((kys, GRID, GRID), F32),
         ((blocks * (2 * HALO_BLK + 1), 4, TILE, TILE), F32),
         ((ext_blocks, 3, TILE, TILE), F32),
@@ -1136,12 +1243,13 @@
         ((ITERS + 1, 3) + tile, F32),
         ((3,) + tile, F32),
         ((ranks, 3) + tile, F32),
-        ((ranks, 3) + tile, F32),
+        ((ranks // 2, 3) + tile, F32),
+        ((ranks // 2, 3) + tile, F32),
         ((1, TILE), F32),
         ((ranks, 1, TILE), F32),
         ((8, GRID), F32),
     ]
-    sems = [dma((2,))] + [dma((ranks,))] * 4 + [dma((2,))] * 2 + [dma((ranks,))] * 2
+    sems = [dma((2,))] + [dma((ranks,))] * 4 + [dma((2,))] * 2 + [dma((ranks // 2,))] * 8
     return buffers, sems
 
 
@@ -1181,7 +1289,7 @@
     constants = [center, eye, along_z(rows.T), along_z(rows), along_x(rows), along_x(rows.T)]
     buffers, sems = fast_shapes(ranks, blocks)
     smem = pl.BlockSpec(memory_space=pltpu.SMEM)
-    return pl.pallas_call(
+    outs = pl.pallas_call(
         functools.partial(fast_kernel, ranks),
         in_specs=[VMEM] * 4 + [smem] * 2 + [VMEM] * len(constants) + [pl.BlockSpec(memory_space=pl.ANY)],
         out_specs=[VMEM] * 2,
@@ -1195,6 +1303,18 @@
         positions, field, inv_polar.reshape(blocks, TILE), x_spline.transpose(1, 0, 2),
         tile_list, tile_count, *[jnp.asarray(c) for c in constants], yz_spline,
     )
+    return pl.pallas_call(
+        finish_kernel,
+        in_specs=[VMEM] * 2,
+        out_specs=[VMEM] * 2,
+        out_shape=[jax.ShapeDtypeStruct(positions.shape, F32)] * 2,
+        name="finish",
+    )(*outs)
+
+
+def finish_kernel(dipoles_in, residual_in, dipoles_out, residual_out):
+    dipoles_out[...] = dipoles_in[...]
+    residual_out[...] = residual_in[...]
 
 
 def solution(mesh):

time: 91.1 us -> 86.1 us (0.945)
  local copies, waits for them, and re-layouts: 2.65 us -> 0 us
  Pallas kernels: 87.4 us -> 85.2 us
    pallas_call x1, Pallas kernels: 87.4 us -> 83.8 us  [fast_device(): pl.pallas_call(functools.partial(fast_kernel, ranks), in_specs=[VMEM] * 4...]
    unnamed x2 -> x0, local copies, waits for them, and re-layouts: 2.65 us -> none
    pallas_call x0 -> x1, Pallas kernels: none -> 1.35 us  [fast_device(): pl.pallas_call(finish_kernel, in_specs=[VMEM] * 2, out_specs=[VMEM] * 2,...]
where the time goes in v3:
time: 86.1 us; the launch traced here: 85.8 us
  Pallas kernels  85.2 us (99%)
    pallas_call x1, Pallas kernels, fast_device(): pl.pallas_call(functools.partial(fast_kernel, ranks), in_specs=[VMEM] * 4...  83.8 us

profile of v3, /device:TPU:0, one launch (start us, length us, event | category | flops | bytes accessed | tf_op | source)
XLA Modules:
  0.0 85.8 jit_solution(17614873047861332746)
XLA Ops:
  0.6 83.8 %induced.1 = (f32[3,1024]{1,0:T(4,128)}, f32[3,1024]{1,0:T(4,128)}) custom-call(f32[3,1024]{1,0:T(4,128)} %pos_ref.1, f32[3,1024]{1,0:T(4,128)} %field_ref.1, f32[8,128]{1,0:T(8,128)} %bitcast.3, f32[5,2,1024]{2,1,0:T(2,128)} %bitcast.2, s32[8,7]{1,0:T(8,128)} %list_ref.1, s32[8]{0:T(128)} %count_ref.1, bf16[256,384]{1,0:T(8,128)(2,1)} %constant.12.clone.center_ref, ...), custom_call_target="tpu_custom_call" | custom-call | tf_op jit(solution)/shard_map/induced/pallas_call | solution.py:1292
  84.5 1.4 %finish.1 = (f32[3,1024]{1,0:T(4,128)}, f32[3,1024]{1,0:T(4,128)}) custom-call(f32[3,1024]{1,0:T(4,128)} %get-tuple-element.4.dipoles_in, f32[3,1024]{1,0:T(4,128)} %get-tuple-element.5.residual_in), custom_call_target="tpu_custom_call" | custom-call | tf_op jit(solution)/shard_map/finish/pallas_call | solution.py:1306

commit v4 on v3

--- a/solution.py
+++ b/solution.py
@@ -561,11 +561,12 @@
 
 def fast_kernel(
     ranks, pos_ref, field_ref, polar_ref, xs_ref, list_ref, count_ref,
-    center_ref, eye_ref, zin_ref, zout_ref, xin_ref, xout_ref, yz_ref,
+    center_ref, eye_in, zin_in, zout_in, xin_in, xout_in, yz_ref,
     dip_ref, res_ref,
+    eye_ref, zin_ref, zout_ref, xin_ref, xout_ref,
     lines, info, table, flipped, yq, xw, wt, wz, vx, mix, hold, grid, spec, wide, low, green, tens, cols, place, sides, ext,
     bases, pair, out_part, pair_part, in_part, part, slots, energy,
-    local_sem, all_send, all_recv, gram_send, gram_recv, side_send, side_recv,
+    local_sem, all_send, all_recv, side_send, side_recv,
     ag_send, ag_recv, on_send, on_recv, pair_send, pair_recv, rs_send, rs_recv,
 ):
     me = lax.axis_index("gx")
@@ -582,6 +583,14 @@
         pltpu.make_async_copy(yz_ref.at[2 * t], lines.at[t], local_sem.at[t]) for t in range(2)
     ]
     for load in loads:
+        load.start()
+    constants = [
+        pltpu.make_async_copy(source, target, local_sem.at[2 + t])
+        for t, (source, target) in enumerate(
+            ((eye_in, eye_ref), (zin_in, zin_ref), (zout_in, zout_ref), (xin_in, xin_ref), (xout_in, xout_ref))
+        )
+    ]
+    for load in constants:
         load.start()
 
     barrier = pltpu.get_barrier_semaphore()
@@ -724,6 +733,9 @@
         lax.fori_loop(low, high, one, 0)
 
     each(1, ranks, lambda d: tell_all(away(d, ranks), me).start())
+    for load in constants:
+        load.wait()
+
     def modes(freq):
         number = jnp.where(freq <= GRID // 2, freq, freq - GRID // 2)
         return number.astype(F32), jnp.where((freq == 0) | (freq == GRID // 2), 1.0 / GRID, 2.0 / GRID)
@@ -757,6 +769,32 @@
             ext[e + HALO_BLK, c : c + 1, :] = place[c, e : e + 1, :]
     with jax.named_scope("poscols"):
         lax.fori_loop(HALO_BLK, HALO_BLK + blocks, position_columns, 0)
+    lag = iota((8, TILE), 1) - iota((8, TILE), 0)
+
+    def tensor(b, k):
+        index = b * reach + k
+        near = jnp.float32(0.0)
+        for s in range(reach):
+            near = jnp.where((list_ref[b, s] == b + k) & (s < count_ref[b]), PAIR_C, near)
+        home = [jnp.broadcast_to(ext[b + HALO_BLK, c : c + 1, :], (8, TILE)) for c in range(3)]
+        hide = jnp.where(k == HALO_BLK, 0, 4 * TILE)
+        for j in range(TILE // 8):
+            rows = slice(8 * j, 8 * j + 8)
+            r = [home[c] - cols[b + k, c, rows, :] for c in range(3)]
+            inverse = lax.rsqrt(r[0] * r[0] + r[1] * r[1] + r[2] * r[2] + 1.0)
+            third = jnp.where(lag != 8 * j + hide, near, 0.0) * inverse * inverse * inverse
+            tens[index, 0, rows, :] = third
+            weight = third * (lax.rsqrt(inverse) * (3.0 / PAIR_C) ** 0.5)
+            for c in range(3):
+                tens[index, 1 + c, rows, :] = weight * r[c]
+
+    def tensors_of(b, low, high):
+        each(low, high, lambda k: tensor(b, k))
+
+    with jax.named_scope("tensors"):
+        each(0, blocks, lambda b: tensors_of(
+            b, jnp.maximum(HALO_BLK - b, 0), jnp.minimum(blocks + HALO_BLK - b, reach)
+        ))
     with jax.named_scope("side_wait"):
         for copy in neighbours:
             copy.wait()
@@ -769,29 +807,9 @@
     with jax.named_scope("poscols2"):
         lax.fori_loop(0, HALO_BLK, position_columns, 0)
         lax.fori_loop(HALO_BLK + blocks, 2 * HALO_BLK + blocks, position_columns, 0)
-    lag = iota((8, TILE), 1) - iota((8, TILE), 0)
-
-    def tensors(index, carry):
-        b, k = index // reach, index % reach
-        near = jnp.float32(0.0)
-        for s in range(reach):
-            near = jnp.where((list_ref[b, s] == b + k) & (s < count_ref[b]), 1.0, near)
-        home = [jnp.broadcast_to(ext[b + HALO_BLK, c : c + 1, :], (8, TILE)) for c in range(3)]
-        hide = jnp.where(k == HALO_BLK, 0, 4 * TILE)
-        for j in range(TILE // 8):
-            rows = slice(8 * j, 8 * j + 8)
-            r = [home[c] - cols[b + k, c, rows, :] for c in range(3)]
-            inverse = lax.rsqrt(r[0] * r[0] + r[1] * r[1] + r[2] * r[2] + 1.0)
-            live = jnp.where(lag != 8 * j + hide, near, 0.0)
-            square = live * inverse * inverse
-            tens[index, 0, rows, :] = PAIR_C * (square * inverse)
-            weight = (3.0 * PAIR_C) ** 0.5 * (square * inverse * lax.rsqrt(inverse))
-            for c in range(3):
-                tens[index, 1 + c, rows, :] = weight * r[c]
-        return carry
-
-    with jax.named_scope("tensors"):
-        lax.fori_loop(0, blocks * reach, tensors, 0)
+    with jax.named_scope("tensors2"):
+        each(0, HALO_BLK, lambda b: tensors_of(b, 0, HALO_BLK - b))
+        each(blocks - HALO_BLK, blocks, lambda b: tensors_of(b, blocks + HALO_BLK - b, reach))
 
     freq = me * kys + iota((kys, TILE), 0)
     sine_mode = freq > GRID // 2
@@ -939,8 +957,8 @@
 
     def tell(i, row):
         return pltpu.make_async_remote_copy(
-            src_ref=part, dst_ref=slots.at[lax.rem(me + row, ranks)], send_sem=gram_send.at[i],
-            recv_sem=gram_recv.at[i], device_id={"gx": lax.rem(me + i, ranks)},
+            src_ref=part, dst_ref=slots.at[lax.rem(me + row, ranks)], send_sem=all_send.at[i],
+            recv_sem=all_recv.at[i], device_id={"gx": lax.rem(me + i, ranks)},
             device_id_type=pl.DeviceIdType.MESH,
         )
 
@@ -1004,6 +1022,17 @@
     def pair_edges():
         each(0, HALO_BLK, lambda b: pair_rows(b, 0, HALO_BLK - b, False))
         each(blocks - HALO_BLK, blocks, lambda b: pair_rows(b, blocks + HALO_BLK - b, reach, False))
+
+    def land(it):
+        with jax.named_scope("rs_wait"):
+            each(1, chips, lambda d: fold(d).wait())
+        for c in range(3):
+            total = out_part[me, c]
+            for i in range(1, chips):
+                total = total + in_part[i, c]
+            following = pair[c] - total
+            bases[it + 1, c] = following
+            info[me, FIELD0 + c] = following / polar_ref[...]
 
     def sweep(it, carry):
         @pl.when(it > 0)
@@ -1152,16 +1181,11 @@
             each(1, chips, lambda d: direct(d).wait_send())
 
         each(0, chips, lambda d: hand_over(d).wait_send())
-        with jax.named_scope("rs_wait"):
-            each(1, chips, lambda d: fold(d).wait())
-        with jax.named_scope("update"):
-            for c in range(3):
-                total = out_part[me, c]
-                for i in range(1, chips):
-                    total = total + in_part[i, c]
-                following = pair[c] - total
-                bases[it + 1, c] = following
-                info[me, FIELD0 + c] = following / polar_ref[...]
+
+        @pl.when(it < ITERS - 1)
+        def _():
+            land(it)
+
         return carry
 
     lax.fori_loop(0, ITERS, sweep, 0)
@@ -1176,11 +1200,13 @@
     sums = {r: jnp.broadcast_to(sums[:, r : r + 1], (1, TILE)) for r in range(last + 1)}
     dipoles, residual = krylov(sums, entries, count)
     for c in range(3):
-        basis = [bases[i, c] for i in range(count)]
-        first = combine(dipoles, [b / polar_ref[...] for b in basis])
-        second = combine(residual, basis)
+        first = combine(dipoles, [bases[i, c] / polar_ref[...] for i in range(ITERS)])
         for b in range(blocks):
             dip_ref[c : c + 1, lanes(b)] = first[b : b + 1, :]
+    land(ITERS - 1)
+    for c in range(3):
+        second = combine(residual, [bases[i, c] for i in range(count)])
+        for b in range(blocks):
             res_ref[c : c + 1, lanes(b)] = second[b : b + 1, :]
 
 
@@ -1249,7 +1275,7 @@
         ((ranks, 1, TILE), F32),
         ((8, GRID), F32),
     ]
-    sems = [dma((2,))] + [dma((ranks,))] * 4 + [dma((2,))] * 2 + [dma((ranks // 2,))] * 8
+    sems = [dma((7,))] + [dma((ranks,))] * 2 + [dma((2,))] * 2 + [dma((ranks // 2,))] * 8
     return buffers, sems
 
 
@@ -1291,10 +1317,11 @@
     smem = pl.BlockSpec(memory_space=pltpu.SMEM)
     outs = pl.pallas_call(
         functools.partial(fast_kernel, ranks),
-        in_specs=[VMEM] * 4 + [smem] * 2 + [VMEM] * len(constants) + [pl.BlockSpec(memory_space=pl.ANY)],
+        in_specs=[VMEM] * 4 + [smem] * 2 + [VMEM] + [pl.BlockSpec(memory_space=pl.ANY)] * len(constants),
         out_specs=[VMEM] * 2,
         out_shape=[jax.ShapeDtypeStruct(positions.shape, F32)] * 2,
-        scratch_shapes=[pltpu.VMEM(s, t) for s, t in buffers] + sems,
+        scratch_shapes=[pltpu.VMEM(c.shape, BF16) for c in constants[1:]]
+        + [pltpu.VMEM(s, t) for s, t in buffers] + sems,
         compiler_params=pltpu.CompilerParams(
             vmem_limit_bytes=62 * 1024 * 1024, collective_id=2, has_side_effects=True
         ),

time: 86.1 us -> 83.4 us (0.969)
  Pallas kernels: 85.2 us -> 82.4 us
    pallas_call x1, Pallas kernels: 83.8 us -> 81 us  [fast_device(): pl.pallas_call(functools.partial(fast_kernel, ranks), in_specs=[VMEM] * 4...]
where the time goes in v4:
time: 83.4 us; the launch traced here: 83 us
  Pallas kernels  82.4 us (99%)
    pallas_call x1, Pallas kernels, fast_device(): pl.pallas_call(functools.partial(fast_kernel, ranks), in_specs=[VMEM] * 4...  81 us

profile of v4, /device:TPU:0, one launch (start us, length us, event | category | flops | bytes accessed | tf_op | source)
XLA Modules:
  0.0 83.0 jit_solution(12647509741723491711)
XLA Ops:
  0.6 81.0 %induced.1 = (f32[3,1024]{1,0:T(4,128)}, f32[3,1024]{1,0:T(4,128)}) custom-call(f32[3,1024]{1,0:T(4,128)} %pos_ref.1, f32[3,1024]{1,0:T(4,128)} %field_ref.1, f32[8,128]{1,0:T(8,128)} %bitcast.3, f32[5,2,1024]{2,1,0:T(2,128)} %bitcast.2, s32[8,7]{1,0:T(8,128)} %list_ref.1, s32[8]{0:T(128)} %count_ref.1, bf16[256,384]{1,0:T(8,128)(2,1)} %constant.12.clone.center_ref, ...), custom_call_target="tpu_custom_call" | custom-call | tf_op jit(solution)/shard_map/induced/pallas_call | solution.py:1318
  81.7 1.4 %finish.1 = (f32[3,1024]{1,0:T(4,128)}, f32[3,1024]{1,0:T(4,128)}) custom-call(f32[3,1024]{1,0:T(4,128)} %get-tuple-element.4.dipoles_in, f32[3,1024]{1,0:T(4,128)} %get-tuple-element.5.residual_in), custom_call_target="tpu_custom_call" | custom-call | tf_op jit(solution)/shard_map/finish/pallas_call | solution.py:1333
